TPU v7x, 512 devices: a whole 4x8x8 slice. The times are simulated.
512 devices in a mesh: section: 4 (over x), ctx: 16 (over z, y_hi), dp: 8 (over y_lo, core).
Axes of the slice: x: 4, y: 8 (y_hi: 2, y_lo: 4; y = y_hi * 4 + y_lo), z: 8, core: 2. Of those that a mesh axis runs over, the one named last changes fastest.
Arguments:
- first_input: bfloat16 [4, 8, 2048, 2048], P('section', 'dp', 'ctx'), may hold values from -14 to 14
- second_input: bfloat16 [4, 8, 2048, 2048], P('section', 'dp', 'ctx'), may hold values from -6 to 6
- upstream: bfloat16 [4, 8, 2048, 2048], P('section', 'dp', 'ctx'), may hold values from -6 to 6
- first_picks: int32 [4, 8, 2048, 6], P('section', 'dp', 'ctx'), may hold values from 0 to 63, all different within a row
- second_picks: int32 [4, 8, 2048, 6], P('section', 'dp', 'ctx'), may hold values from 0 to 63, all different within a row
- gate_grads: float32 [4, 8, 2048, 6], P('section', 'dp', 'ctx'), may hold values from -0.0009 to 0.0009
- norm_gain: float32 [4, 2048], P('section'), may hold values from 0.5 to 1.5
- router_weight: float32 [4, 64, 2048], P('section'), may hold values from -0.25 to 0.25
- gate_weight: bfloat16 [4, 2048, 1280], P('section', 'ctx'), may hold values from -0.125 to 0.125
- up_weight: bfloat16 [4, 2048, 1280], P('section', 'ctx'), may hold values from -0.125 to 0.125
- down_weight: bfloat16 [4, 1280, 2048], P('section', None, 'ctx'), may hold values from -0.15625 to 0.15625
Outputs:
- arrived: bfloat16 [4, 8, 2048, 2048], P('section', 'dp', 'ctx')
- routing: float32 [4, 8, 2048, 6], P('section', 'dp', 'ctx')
- input_grad: bfloat16 [4, 8, 2048, 2048], P('section', 'dp', 'ctx')
- router_grad: float32 [4, 64, 2048], P('section')
- balance: float32 [4, 8, 2], P('section', 'dp')
Inputs may be any that keep to these rules, and one draw needn't show every extreme that they name: `first_picks`: each token names 6 different experts. `second_picks`: each token names 6 different experts.
All inputs are finite; a program needn't handle non-finite values.
Results may differ from a plain program's by a relative error of at most 0.002.
The roundings to bfloat16 on the way count: a program that leaves them out, or rounds other values in their place, can miss the bound.
Values may be sent and summed in bfloat16 or wider, within the bound.
A program may use at most 64 MiB of HBM per device.

v0:
```python
import jax
import jax.numpy as jnp
from jax import lax
from jax.sharding import Mesh
from jax.sharding import PartitionSpec as P

CTX = ("ctx_0", "ctx_1")
CTX_DP = ("ctx_0", "ctx_1", "dp")


EPSILON = 1e-06
ROUTE_SCALE = 2.5


def shifted(block, axis, distance):
    devices = range(lax.axis_size(axis))
    route = [((i - distance) % len(devices), i) for i in devices]
    return lax.ppermute(block, axis, route)


def sent_to_all(array, axis):
    size = lax.axis_size(axis)
    return lax.all_to_all(
        jnp.broadcast_to(array[None], (size, *array.shape)), axis, 0, 0, tiled=True
    )


def over_copies(array, axis):
    everything = sent_to_all(array, axis)
    return jnp.sum(everything, axis=0)


def packed_total(arrays, axis):
    ends = [0]
    for a in arrays:
        ends.append(ends[-1] + a.size)
    subtotal = over_copies(jnp.concatenate([a.ravel() for a in arrays]), axis)
    return tuple((subtotal[b:e].reshape(a.shape) for a, b, e in zip(arrays, ends, ends[1:])))


def sent_together(arrays, axis, dim, along):
    ends, at = ([], 0)
    for a in arrays[:-1]:
        at += a.shape[along]
        ends.append(at)
    both = jnp.concatenate(arrays, axis=along)
    return tuple(jnp.split(lax.all_gather(both, axis, axis=dim, tiled=True), ends, axis=along))


def gather_axes(array, axes, dim):
    for axis in reversed(axes):
        array = lax.all_gather(array, axis, axis=dim, tiled=True)
    return array


def normalize(values_in, norm_gain):
    values = values_in.astype(jnp.float32)
    inverse = lax.rsqrt(jnp.mean(values * values, axis=-1, keepdims=True) + EPSILON)
    return ((values * inverse * norm_gain).astype(jnp.bfloat16), inverse)


def one_hot(picks, experts):
    labels = jnp.arange(experts, dtype=jnp.int32)
    return (picks[:, :, None] == labels[None, None, :]).astype(jnp.float32)


def scores(normed, router_w, table):
    logits = jnp.dot(normed.astype(jnp.float32), router_w.T, precision=lax.Precision.HIGHEST)
    affinity = jax.nn.sigmoid(logits)
    chosen = jnp.einsum("tke,te->tk", table, affinity, precision=lax.Precision.HIGHEST)
    chosen_sum = jnp.sum(chosen, axis=-1, keepdims=True)
    gate_weights = ROUTE_SCALE * chosen / chosen_sum
    spread = jnp.sum(affinity, axis=-1, keepdims=True)
    shares = affinity / spread
    return (affinity, chosen, chosen_sum, gate_weights, spread, shares)


def router_back(grads, table, affinity, chosen, chosen_sum, spread, shares, frac, length):
    chosen_grad = ROUTE_SCALE * (
        grads / chosen_sum
        - jnp.sum(grads * chosen, axis=-1, keepdims=True) / (chosen_sum * chosen_sum)
    )
    affinity_grad = jnp.einsum("tk,tke->te", chosen_grad, table, precision=lax.Precision.HIGHEST)
    share_grad = frac[None, :] / length
    affinity_grad = (
        affinity_grad + (share_grad - jnp.sum(share_grad * shares, axis=-1, keepdims=True)) / spread
    )
    return affinity_grad * affinity * (1.0 - affinity)


def shared_back(hidden_grad, gate_pre, up_pre):
    sigmoid_v = jax.nn.sigmoid(gate_pre)
    slope = sigmoid_v * (1.0 + gate_pre * (1.0 - sigmoid_v))
    gate_grad = (hidden_grad * up_pre * slope).astype(jnp.bfloat16)
    up_grad = (hidden_grad * gate_pre * sigmoid_v).astype(jnp.bfloat16)
    return (gate_grad, up_grad)


def norm_back(values_in, inverse, norm_gain, normed_grad):
    values = values_in.astype(jnp.float32)
    scaled = normed_grad * norm_gain
    return inverse * (
        scaled - values * inverse * inverse * jnp.mean(scaled * values, axis=-1, keepdims=True)
    )


def shards(
    first_input,
    second_input,
    upstream,
    first_picks,
    second_picks,
    gate_grads,
    norm_gain,
    router_weight,
    gate_weight,
    up_weight,
    down_weight,
):
    first_in = first_input[0, 0]
    second_in = second_input[0, 0]
    first_pk = first_picks[0, 0]
    second_pk = second_picks[0, 0]
    grads = gate_grads[0, 0]
    gain_s = norm_gain[0]
    router_w = router_weight[0]
    experts = router_w.shape[0]
    tokens = first_in.shape[0]
    per_token = first_pk.shape[1]
    length = tokens * lax.axis_size(CTX)
    table_a = one_hot(first_pk, experts)
    table_b = one_hot(second_pk, experts)
    counts_a = jnp.sum(table_a, axis=(0, 1))
    counts_b = jnp.sum(table_b, axis=(0, 1))
    returned = shifted(upstream[0, 0], "section", -1)
    normed_a, inverse_a = normalize(first_in, gain_s)
    normed_b, inverse_b = normalize(second_in, gain_s)
    aff_a, chosen_a, csum_a, routing_a, spread_a, shares_a = scores(normed_a, router_w, table_a)
    aff_b, chosen_b, csum_b, routing_b, spread_b, shares_b = scores(normed_b, router_w, table_b)
    sums_a = jnp.sum(shares_a, axis=0)
    sums_b = jnp.sum(shares_b, axis=0)
    counts_a, counts_b, sums_a, sums_b = packed_total((counts_a, counts_b, sums_a, sums_b), CTX)
    frac_a = experts / (per_token * length) * counts_a
    frac_b = experts / (per_token * length) * counts_b
    balance = jnp.stack([jnp.sum(frac_a * sums_a / length), jnp.sum(frac_b * sums_b / length)])
    stacked = jnp.concatenate([normed_a, normed_b], axis=0)
    gate_rows, up_rows = sent_together((gate_weight[0], up_weight[0]), CTX, 0, 1)
    gate_acc = jnp.dot(stacked, gate_rows, preferred_element_type=jnp.float32)
    up_acc = jnp.dot(stacked, up_rows, preferred_element_type=jnp.float32)
    hidden = (jax.nn.silu(gate_acc) * up_acc).astype(jnp.bfloat16)
    hidden_a = hidden[:tokens]
    columns = gather_axes(down_weight[0], CTX, 1)
    out_acc = jnp.dot(hidden_a, columns, preferred_element_type=jnp.float32)
    grad_acc = jnp.einsum("td,fd->tf", returned, columns, preferred_element_type=jnp.float32)
    output_a = (first_in.astype(jnp.float32) + out_acc).astype(jnp.bfloat16)
    arrived = shifted(output_a, "section", 1)
    gate_grad, up_grad = shared_back(grad_acc, gate_acc[tokens:], up_acc[tokens:])
    normed_grad = jnp.einsum("tf,df->td", gate_grad, gate_rows, preferred_element_type=jnp.float32)
    normed_grad = normed_grad + jnp.einsum(
        "tf,df->td", up_grad, up_rows, preferred_element_type=jnp.float32
    )
    logit_grad = router_back(
        grads, table_b, aff_b, chosen_b, csum_b, spread_b, shares_b, frac_b, length
    )
    router_part = jnp.dot(
        logit_grad.T, normed_b.astype(jnp.float32), precision=lax.Precision.HIGHEST
    )
    normed_grad = normed_grad + jnp.dot(logit_grad, router_w, precision=lax.Precision.HIGHEST)
    input_grad = (
        returned.astype(jnp.float32) + norm_back(second_in, inverse_b, gain_s, normed_grad)
    ).astype(jnp.bfloat16)
    router_total = lax.psum(router_part, CTX_DP)
    return (
        arrived[None, None],
        routing_a[None, None],
        input_grad[None, None],
        router_total[None],
        balance[None, None],
    )


def solution(mesh):
    split = Mesh(
        mesh.devices.reshape(mesh.shape["section"], 8, 2, mesh.shape["dp"]),
        ("section", "ctx_0", "ctx_1", "dp"),
    )
    return jax.shard_map(
        shards,
        mesh=split,
        in_specs=(
            P("section", "dp", CTX, None),
            P("section", "dp", CTX, None),
            P("section", "dp", CTX, None),
            P("section", "dp", CTX, None),
            P("section", "dp", CTX, None),
            P("section", "dp", CTX, None),
            P("section", None),
            P("section", None, None),
            P("section", CTX, None),
            P("section", CTX, None),
            P("section", None, CTX),
        ),
        out_specs=(
            P("section", "dp", CTX, None),
            P("section", "dp", CTX, None),
            P("section", "dp", CTX, None),
            P("section", None, None),
            P("section", "dp", None),
        ),
        check_vma=False,
    )
```

profile of v0, /device:TPU:57, one launch (start us, length us, event | category | flops | bytes accessed | tf_op | source)
XLA Modules:
  0.0 400.5 jit_solution(3876128680770797698)
XLA Ops:
  8.0 0.0 copy-start
  8.0 0.0 copy-start.8
  8.1 0.0 all-gather.7.cloned.1.call-start
  8.1 16.5 %all-gather = bf16[1,1280,256]{2,1,0:T(8,128)(2,1)} all-gather(bf16[1,1280,128]{2,1,0:T(8,128)(2,1)} %param.21), channel_id=2, replica_groups=mesh['section'=4,'ctx_0'=8,'ctx_1'=2,'dp'=8] {'ctx_1'}, dimensions={2}, use_global_device_ids=true | all-gather | bytes 983040 | tf_op jit(solution)/shard_map/all_gather | solution.py:52
  24.6 0.0 all-gather.7.cloned.1.call-update
  24.6 0.0 all-gather.5.cloned.1.call-start
  24.7 2.0 pad_maximum_fusion.3
  26.7 0.0 all-gather.5.cloned.1.call-update
  26.7 4.4 %collective-permute-start.1 = (bf16[128,2048]{1,0:T(8,128)(2,1)S(1)}, bf16[128,2048]{1,0:T(8,128)(2,1)S(1)}, u32[]{:S(2)}, u32[]{:S(2)}) collective-permute-start(bf16[128,2048]{1,0:T(8,128)(2,1)S(1)} %bitcast.131), channel_id=1, source_target_pairs={{128,0},{256,128},{384,256},{0,384},{129,1},{257,129},{385,257},{1... | collective-permute-start | bytes 1572872 | tf_op jit(solution)/shard_map/ppermute | solution.py:18
  31.2 0.2 fusion.44
  31.4 0.8 fusion.84
  32.2 0.1 convert_reduce_fusion.1
  32.4 0.1 convert_reduce_fusion
  32.5 0.2 fusion.39
  32.7 0.8 fusion.83
  33.5 0.1 fusion.72
  33.6 0.1 pad_maximum_fusion.4
  33.7 0.6 broadcast_in_dim.14
  34.3 15.1 %all-to-all-start = ((f32[16,1,256]{2,1,0:T(1,128)}), f32[16,1,256]{2,1,0:T(1,128)S(1)}, u32[]{:S(2)}, u32[]{:S(2)}) async-start(f32[16,1,256]{2,1,0:T(1,128)} %broadcast_in_dim.14), calls=%async_computation | async-start | bytes 32768 | tf_op jit(solution)/shard_map/all_to_all | solution.py:23
  49.4 0.0 all-reduce.2.cloned.1.call-start
  49.6 1.0 fusion.41
  50.5 0.6 broadcast_in_dim.13
  51.1 5.1 %all-to-all-done = f32[16,1,256]{2,1,0:T(1,128)S(1)} async-done(((f32[16,1,256]{2,1,0:T(1,128)}), f32[16,1,256]{2,1,0:T(1,128)S(1)}, u32[]{:S(2)}, u32[]{:S(2)}) %all-to-all-start) | async-done | bytes 16416 | tf_op jit(solution)/shard_map/all_to_all | solution.py:23
  56.2 0.6 multiply_reduce_fusion.2
  56.9 0.1 multiply_reduce_fusion
  57.0 1.2 convolution_bitcast_fusion
  58.2 0.0 all-reduce.2.cloned.1.call-update
  58.2 1.8 maximum_bitcast_fusion
  60.0 0.0 collective-permute-done.1
  60.0 44.6 %all-gather.7.cloned.1.call-done = bf16[1,1280,2048]{2,1,0:T(8,128)(2,1)} async-done(((bf16[1,1280,256]{2,1,0:T(8,128)(2,1)}), bf16[1,1280,2048]{2,1,0:T(8,128)(2,1)}) %all-gather.7.cloned.1.call-update) | async-done | bytes 5242896 | tf_op jit(solution)/shard_map/all_gather | solution.py:52
  104.6 4.4 %fusion = f32[128,1280]{1,0:T(8,128)S(1)} fusion(bf16[128,2048]{1,0:T(8,128)(2,1)S(1)} %collective-permute-done.1, bf16[1,1280,2048]{2,1,0:T(8,128)(2,1)} %all-gather.7.cloned.1.call-done), kind=kOutput, calls=%fused_computation | convolution fusion | flops 671088640 | bytes 6422528 | tf_op jit(solution)/shard_map/td,fd->tf/dot_general | solution.py:154
  109.0 215.8 %all-gather.5.cloned.1.call-done = bf16[2048,2560]{1,0:T(8,128)(2,1)} async-done(((bf16[128,2560]{1,0:T(8,128)(2,1)}), bf16[2048,2560]{1,0:T(8,128)(2,1)}) %all-gather.5.cloned.1.call-update) | async-done | bytes 10485776 | tf_op jit(solution)/shard_map/all_gather | solution.py:47
  324.8 4.3 %fusion.6 = f32[256,1280]{1,0:T(8,128)S(1)} fusion(bf16[2048,2560]{1,0:T(8,128)(2,1)} %all-gather.5.cloned.1.call-done, bf16[128,2048]{1,0:T(8,128)(2,1)S(1)} %get-tuple-element.16, bf16[128,2048]{1,0:T(8,128)(2,1)} %get-tuple-element.15), kind=kOutput, calls=%fused_computation.6 | convolution fusion | flops 1344274432 | bytes 7602176 | tf_op jit(solution)/shard_map/dot_general | solution.py:149
  329.1 0.0 slice-start.1
  329.1 0.0 slice-start.2
  329.2 0.0 slice-start.3
  329.2 4.2 %fusion.85 = (f32[256,1280]{1,0:T(8,128)S(1)}, f32[256,1280]{1,0:T(8,128)S(1)}) fusion(bf16[2048,2560]{1,0:T(8,128)(2,1)} %all-gather.5.cloned.1.call-done, bf16[128,2048]{1,0:T(8,128)(2,1)S(1)} %get-tuple-element.16, bf16[128,2048]{1,0:T(8,128)(2,1)S(1)} %copy-done.3), kind=kOutput, calls=%fused_computation.118 | convolution fusion | flops 1344602112 | bytes 8912896 | tf_op jit(solution)/shard_map/dot_general | solution.py:148
  333.4 0.0 slice-start.4
  333.4 1.0 fusion.19
  334.4 2.0 collective-permute-start
  336.5 1.8 fusion.4
  338.3 1.8 fusion.16
  340.1 1.3 fusion.45
  341.5 1.2 fusion.57
  342.7 6.7 %collective-permute-done = bf16[128,2048]{1,0:T(8,128)(2,1)S(1)} collective-permute-done((bf16[128,2048]{1,0:T(8,128)(2,1)S(1)}, bf16[128,2048]{1,0:T(8,128)(2,1)S(1)}, u32[]{:S(2)}, u32[]{:S(2)}) %collective-permute-start) | collective-permute-done | bytes 524320 | tf_op jit(solution)/shard_map/ppermute | solution.py:18
  349.4 41.1 %all-reduce.2.cloned.1.call-done = f32[1,64,2048]{2,1,0:T(8,128)} async-done(((f32[1,64,2048]{2,1,0:T(8,128)}), f32[1,64,2048]{2,1,0:T(8,128)}) %all-reduce.2.cloned.1.call-update) | async-done | bytes 524304 | tf_op jit(solution)/shard_map/psum | solution.py:172
  390.4 0.8 copy.62
  391.2 1.9 copy.63
  (37 shorter events, 0.2 us)
Async XLA Ops:
  8.0 23.4 %copy-start = (f32[1,64,2048]{2,1,0:T(8,128)S(1)}, f32[1,64,2048]{2,1,0:T(8,128)}, u32[]{:S(2)}) copy-start(f32[1,64,2048]{2,1,0:T(8,128)} %param.18) | copy-start | bytes 1572868
  8.0 18.7 %copy-start.8 = (bf16[1,1,128,2048]{3,2,1,0:T(8,128)(2,1)S(1)}, bf16[1,1,128,2048]{3,2,1,0:T(8,128)(2,1)}, u32[]{:S(2)}) copy-start(bf16[1,1,128,2048]{3,2,1,0:T(8,128)(2,1)} %param.13) | copy-start | bytes 1572868
  8.0 23.1 %copy-start.6 = (s32[1,1,128,6]{2,1,3,0:T(1,128)S(1)}, s32[1,1,128,6]{2,1,3,0:T(1,128)}, u32[]{:S(2)}) copy-start(s32[1,1,128,6]{2,1,3,0:T(1,128)} %param.14) | copy-start | bytes 9220
  8.0 23.1 %copy-start.7 = (s32[1,1,128,6]{2,1,3,0:T(1,128)S(1)}, s32[1,1,128,6]{2,1,3,0:T(1,128)}, u32[]{:S(2)}) copy-start(s32[1,1,128,6]{2,1,3,0:T(1,128)} %param.15) | copy-start | bytes 9220
  8.0 23.1 %copy-start.1 = (bf16[1,1,128,2048]{3,2,1,0:T(8,128)(2,1)S(1)}, bf16[1,1,128,2048]{3,2,1,0:T(8,128)(2,1)}, u32[]{:S(2)}) copy-start(bf16[1,1,128,2048]{3,2,1,0:T(8,128)(2,1)} %param.12) | copy-start | bytes 1572868
  8.1 23.3 %copy-start.4 = (f32[1,2048]{1,0:T(1,128)S(1)}, f32[1,2048]{1,0:T(1,128)}, u32[]{:S(2)}) copy-start(f32[1,2048]{1,0:T(1,128)} %param.17) | copy-start | bytes 24580
  8.1 96.5 %all-gather.7.cloned.1.call-start = ((), (), s32[]{:S(2)}) async-start(), calls=%async_computation.3 | async-start | bytes 5898240 | tf_op jit(solution)/shard_map/all_gather | solution.py:52
  24.6 7.6 %copy-start.5 = (f32[1,1,128,6]{2,1,3,0:T(1,128)S(1)}, f32[1,1,128,6]{2,1,3,0:T(1,128)}, u32[]{:S(2)}) copy-start(f32[1,1,128,6]{2,1,3,0:T(1,128)} %param.16) | copy-start | bytes 9220
  24.6 7.9 %copy-start.2 = (bf16[1,1,128,2048]{3,2,1,0:T(8,128)(2,1)S(1)}, bf16[1,1,128,2048]{3,2,1,0:T(8,128)(2,1)}, u32[]{:S(2)}) copy-start(bf16[1,1,128,2048]{3,2,1,0:T(8,128)(2,1)} %param.11) | copy-start | bytes 1572868
  24.6 300.2 %all-gather.5.cloned.1.call-start = ((), (), s32[]{:S(2)}) async-start(), calls=%async_computation.1 | async-start | bytes 11141120 | tf_op jit(solution)/shard_map/all_gather | solution.py:47
  26.7 33.3 %collective-permute-start.1 = (bf16[128,2048]{1,0:T(8,128)(2,1)S(1)}, bf16[128,2048]{1,0:T(8,128)(2,1)S(1)}, u32[]{:S(2)}, u32[]{:S(2)}) collective-permute-start(bf16[128,2048]{1,0:T(8,128)(2,1)S(1)} %bitcast.131), channel_id=1, source_target_pairs={{128,0},{256,128},{384,256},{0,384},{129,1},{257,129},{385,257},{1... | collective-permute-start | bytes 1572872 | tf_op jit(solution)/shard_map/ppermute | solution.py:18
  34.3 21.9 %all-to-all-start = ((f32[16,1,256]{2,1,0:T(1,128)}), f32[16,1,256]{2,1,0:T(1,128)S(1)}, u32[]{:S(2)}, u32[]{:S(2)}) async-start(f32[16,1,256]{2,1,0:T(1,128)} %broadcast_in_dim.14), calls=%async_computation | async-start | bytes 32768 | tf_op jit(solution)/shard_map/all_to_all | solution.py:23
  49.4 341.0 %all-reduce.2.cloned.1.call-start = ((), (), s32[]{:S(2)}) async-start(), calls=%async_computation.2 | async-start | bytes 1048576 | tf_op jit(solution)/shard_map/psum | solution.py:172
  324.8 4.3 %copy-start.3 = (bf16[128,2048]{1,0:T(8,128)(2,1)S(1)}, bf16[128,2048]{1,0:T(8,128)(2,1)}, u32[]{:S(2)}) copy-start(bf16[128,2048]{1,0:T(8,128)(2,1)} %get-tuple-element.15) | copy-start | bytes 1572868
  324.8 8.5 %slice-start = ((s8[5242880]{0:T(1024)(128)(4,1)}), s8[4194304]{0:T(1024)(128)(4,1)S(1)}, s32[]{:S(2)}) async-start(s8[5242880]{0:T(1024)(128)(4,1)} %bitcast.116), calls=%async_computation.4 | async-start | bytes 8388608
  329.1 4.2 %slice-start.1 = ((s8[5242880]{0:T(1024)(128)(4,1)}), s8[1048576]{0:T(1024)(128)(4,1)S(1)}, s32[]{:S(2)}) async-start(s8[5242880]{0:T(1024)(128)(4,1)} %bitcast.116), calls=%async_computation.5 | async-start | bytes 2097152
  329.1 7.3 %slice-start.2 = ((s8[10485760]{0:T(1024)(128)(4,1)}), s8[4194304]{0:T(1024)(128)(4,1)S(1)}, s32[]{:S(2)}) async-start(s8[10485760]{0:T(1024)(128)(4,1)} %bitcast.129), calls=%async_computation.6 | async-start | bytes 8388608
  329.2 7.3 %slice-start.3 = ((s8[10485760]{0:T(1024)(128)(4,1)}), s8[4194304]{0:T(1024)(128)(4,1)S(1)}, s32[]{:S(2)}) async-start(s8[10485760]{0:T(1024)(128)(4,1)} %bitcast.129), calls=%async_computation.7 | async-start | bytes 8388608
  333.4 3.1 slice-start.4
  334.4 15.0 %collective-permute-start = (bf16[128,2048]{1,0:T(8,128)(2,1)S(1)}, bf16[128,2048]{1,0:T(8,128)(2,1)S(1)}, u32[]{:S(2)}, u32[]{:S(2)}) collective-permute-start(bf16[128,2048]{1,0:T(8,128)(2,1)S(1)} %fusion.19), channel_id=1, source_target_pairs={{384,0},{0,128},{128,256},{256,384},{385,1},{1,129},{129,257},{257... | collective-permute-start | bytes 1572872 | tf_op jit(solution)/shard_map/ppermute | solution.py:18
Sparse Core Ops, SparseCore 0:
  24.7 79.8 all-gather.6
  107.8 216.9 all-gather.4
Sparse Core Ops, SparseCore 1:
  58.3 332.1 all-reduce.1
where the time goes:
time: 404 us; the launch traced here: 401 us
  waiting for transfers between devices  313 us (77%)
  starting transfers between devices  21.7 us (5%)
  matrix products  21.6 us (5%)
  blocking collectives  16.5 us (4%)
  between operations  15.8 us (4%)
  other arithmetic  7.71 us (2%)
    all_gather x1, waiting for transfers between devices, sent_together(): lax.all_gather(both, axis, axis=dim, tiled=True)  216 us
    all_gather x1, waiting for transfers between devices, gather_axes(): array = lax.all_gather(array, axis, axis=dim, tiled=True)  44.6 us
    psum x1, waiting for transfers between devices, shards(): router_total = lax.psum(router_part, CTX_DP)  41.1 us
    all_gather x1, blocking collectives, gather_axes(): array = lax.all_gather(array, axis, axis=dim, tiled=True)  16.5 us
    all_to_all x1, starting transfers between devices, sent_to_all(): lax.all_to_all(jnp.broadcast_to(array[None], (size, *array.shape)), axis,...  15.1 us
  transfers between devices with their start and end apart: 6, of which 5 were waited for; matrix products, arithmetic and copies ran while one was open for 8% of the time, Pallas kernels for 0%

commit v1 on v0

v1 whole, which is shorter than its diff:
```python
import jax
import jax.numpy as jnp
from jax import lax
from jax.experimental import pallas as pl
from jax.experimental.pallas import tpu as pltpu
from jax.sharding import Mesh
from jax.sharding import PartitionSpec as P

CTX = ("ctx_0", "ctx_1")
MESH = pl.DeviceIdType.MESH
EPSILON = 1e-06
ROUTE_SCALE = 2.5
HIGH = lax.Precision.HIGHEST
F32 = jnp.float32
BF16 = jnp.bfloat16

NZ, NY, NX = 8, 8, 4
GZ, DZ = 14, 7
GY, DY = 16, 8
NZP, NYP = GZ + DZ, GY + DY
LA, LB = 1, 2

NT = (((1,), (1,)), ((), ()))
TN = (((0,), (0,)), ((), ()))
NN = (((1,), (0,)), ((), ()))


def dot(a, b, dims=NN, precision=None):
    return lax.dot_general(a, b, dims, precision=precision, preferred_element_type=F32)


def sigmoid(v):
    return jax.nn.sigmoid(v)


def kernel(
    first, second, upstream, picks_a, picks_b, grads, gain, router_w, gate, up, down,
    arrived, routing, input_grad, router_grad, balance,
    wgu, wd, returned, normed, inverse, gacc, uacc, hgrad, hid, gg, ug, out, qbuf,
    cnt_src, cnt, aff, csum, spread, logit,
    rp, r0, b0, b1, r1, b2, r2, r3,
    local_sem, zsend, zrecv, ysend, yrecv, dzsend, dzrecv, dysend, dyrecv,
    xsem, osend, orecv, csend, crecv, rsend, rrecv,
):
    d_model = gate.shape[0] * 2 * NZ
    hidden = gate.shape[1]
    tokens = first.shape[0]
    rows_s = gate.shape[0]
    pg, pd = rows_s // 4, hidden // 2
    block = 2 * rows_s
    length = tokens * 2 * NZ

    x = lax.axis_index("section")
    z = lax.axis_index("ctx_0")
    h = lax.axis_index("ctx_1")
    dp = lax.axis_index("dp")
    j = dp // 2
    c = dp % 2
    y = h * 4 + j
    sgn = 1 - 2 * c

    def dev(xx, zz, yy, cc):
        return (xx, zz, yy // 4, (yy % 4) * 2 + cc)

    partner = dev(x, z, y, 1 - c)
    z_next = dev(x, (z + sgn + NZ) % NZ, y, c)
    y_next = dev(x, z, (y + sgn + NY) % NY, c)
    x_next = dev((x + 1) % NX, z, y, c)
    x_prev = dev((x + NX - 1) % NX, z, y, c)

    def z_peer(r):
        return dev(x, (z + r) % NZ, y, c)

    def y_peer(r):
        return dev(x, z, (y + r) % NY, c)

    def c_peer(r):
        rank = (z * 2 + h + r) % (2 * NZ)
        return (x, rank // 2, rank % 2, dp)

    def remote(src, dst, send, recv, device):
        return pltpu.make_async_remote_copy(
            src_ref=src, dst_ref=dst, send_sem=send, recv_sem=recv, device_id=device, device_id_type=MESH
        )

    barrier = pltpu.get_barrier_semaphore()

    def greet(device):
        pl.semaphore_signal(barrier, inc=1, device_id=device, device_id_type=MESH)

    greet(partner)
    greet(x_next)
    greet(x_prev)
    for r in range(1, 2 * NZ):
        greet(c_peer(r))
    for r in range(1, NY):
        if r != 4:
            greet(y_peer(r))

    own = z * 2 + h
    own_rows = pl.ds(pl.multiple_of(own * rows_s, rows_s), rows_s)
    local = [
        pltpu.make_async_copy(gate, wgu.at[0, own_rows, :], local_sem.at[0]),
        pltpu.make_async_copy(up, wgu.at[1, own_rows, :], local_sem.at[1]),
        pltpu.make_async_copy(down, wd.at[:, own_rows], local_sem.at[2]),
    ]
    for copy in local:
        copy.start()
    for copy in local:
        copy.wait()
    pl.semaphore_wait(barrier, 3 + 2 * NZ - 1 + NY - 2)

    def g_piece(slot, p):
        start = pl.multiple_of(slot * rows_s + p * pg, pg)
        return wgu.at[:, pl.ds(start, pg), :]

    def d_piece(slot, p):
        return wd.at[pl.ds(pl.multiple_of(p * pd, pd), pd), pl.ds(pl.multiple_of(slot * rows_s, rows_s), rows_s)]

    def slot_of(zz, hh):
        return ((zz + 2 * NZ) % NZ) * 2 + hh

    def zg_ref(n, core, sign):
        return g_piece(slot_of(z - sign * (n // 4 + 1), h), (2 * core + n % 4) % 4)

    def zd_ref(n, core, sign):
        return d_piece(slot_of(z - sign * (n // 2 + 1), h), (core + n % 2) % 2)

    def y_offset(q, sign):
        return (1 - 2 * (q % 2)) * ((q + 1) // 2) * sign

    def yg_ref(n, core, sign, hh):
        return g_piece(slot_of(z + y_offset(n // 2, sign), hh), 2 * core + n % 2)

    def yd_ref(n, core, sign, hh):
        return d_piece(slot_of(z + y_offset(n, sign), hh), core)

    def zg_send(n):
        ref = g_piece(slot_of(z - sgn * (n // 4), h), (2 * c + n % 4) % 4)
        return remote(ref, ref, zsend.at[n], zrecv.at[n], z_next)

    def zd_send(n):
        ref = d_piece(slot_of(z - sgn * (n // 2), h), (c + n % 2) % 2)
        return remote(ref, ref, zsend.at[GZ + n], zrecv.at[GZ + n], z_next)

    last = 3 * (1 - c)
    is_last = j == last
    hops = jnp.where(c == 0, j + 1, 4 - j)
    hops_max = jnp.maximum(hops, 5 - hops)
    send_half = jnp.where(is_last, h, 1 - h)

    def yg_send(n):
        ref = yg_ref(n, c, sgn, send_half)
        return remote(ref, ref, ysend.at[n], yrecv.at[n], y_next)

    def yd_send(n):
        ref = yd_ref(n, c, sgn, send_half)
        return remote(ref, ref, ysend.at[GY + n], yrecv.at[GY + n], y_next)

    for n in range(4):
        zg_send(n).start()

    @pl.when(is_last)
    def _():
        for n in range(2):
            yg_send(n).start()

    back = remote(upstream, returned, xsem.at[0], xsem.at[1], x_prev)
    back.start()

    step_rows = 16

    def norm_rows(source, base):
        def body(i, _):
            rows = pl.ds(pl.multiple_of(i * step_rows, step_rows), step_rows)
            values = source[rows, :].astype(F32)
            inv = lax.rsqrt(jnp.mean(values * values, axis=-1, keepdims=True) + EPSILON)
            inverse[pl.ds(pl.multiple_of(base + i * step_rows, step_rows), step_rows), :] = jnp.broadcast_to(inv, (step_rows, 128))
            scaled = (values * inv * gain[...]).astype(BF16)
            for b in range(d_model // block):
                normed[b, pl.ds(pl.multiple_of(base + i * step_rows, step_rows), step_rows), :] = scaled[:, b * block : (b + 1) * block]
            return 0

        lax.fori_loop(0, tokens // step_rows, body, 0)

    norm_rows(first, 0)
    norm_rows(second, tokens)
    gacc[...] = jnp.zeros_like(gacc)
    uacc[...] = jnp.zeros_like(uacc)
    hgrad[...] = jnp.zeros_like(hgrad)

    experts = router_w.shape[0]
    top = picks_a.shape[0]
    logits = jnp.zeros((experts, 2 * tokens), F32)
    for b in range(d_model // block):
        logits = logits + dot(
            router_w[:, b * block : (b + 1) * block], normed[b].astype(F32), NT, HIGH
        )
    affinity = sigmoid(logits)
    aff[...] = affinity
    labels = lax.broadcasted_iota(jnp.int32, (experts, tokens), 0)

    def picked(picks, affinities, k):
        hit = picks[k : k + 1, :] == labels
        return jnp.sum(jnp.where(hit, affinities, 0.0), axis=0, keepdims=True), hit

    stats = []
    for m, picks in enumerate((picks_a, picks_b)):
        part = affinity[:, m * tokens : (m + 1) * tokens]
        tab = jnp.zeros((experts, tokens), F32)
        chosen = []
        for k in range(top):
            value, hit = picked(picks, part, k)
            chosen.append(value)
            tab = tab + jnp.where(hit, 1.0, 0.0)
        total = chosen[0]
        for value in chosen[1:]:
            total = total + value
        all_aff = jnp.sum(part, axis=0, keepdims=True)
        if m == 0:
            for k in range(top):
                routing[k : k + 1, :] = ROUTE_SCALE * chosen[k] / total
        else:
            csum[...] = total
            spread[...] = all_aff
        stats.append((tab, part / all_aff))
    ones = jnp.ones((8, tokens), F32)
    counts_row = dot(ones, jnp.concatenate([stats[0][0], stats[1][0]], axis=0), NT, HIGH)
    shares_row = dot(ones, jnp.concatenate([stats[0][1], stats[1][1]], axis=0), NT, HIGH)
    row_id = lax.broadcasted_iota(jnp.int32, (8, 2 * experts), 0)
    packed = jnp.where(row_id == 0, counts_row, jnp.where(row_id == 1, shares_row, 0.0))
    cnt_src[...] = packed
    for r in range(1, 2 * NZ):
        remote(cnt_src, cnt.at[r], csend.at[r], crecv.at[r], c_peer(r)).start()

    half_e = experts // 2
    own_half = pl.ds(pl.multiple_of(c * half_e, half_e), half_e)
    other_half = pl.ds(pl.multiple_of((1 - c) * half_e, half_e), half_e)

    def cols(i, width):
        return pl.ds(pl.multiple_of(i * width, width), width)

    def rs_pair():
        return remote(rp.at[other_half, :], b0, rsend.at[0], rrecv.at[0], partner)

    def rs_z(r):
        return remote(
            r0.at[:, cols((z + r) % NZ, block)], b1.at[r], rsend.at[r], rrecv.at[r], z_peer(r)
        )

    def tile(yy):
        return (cols(yy // 2, 8), cols(yy % 2, 128))

    def rs_y(r):
        return remote(r1.at[tile((y + r) % NY)], b2.at[r], rsend.at[8 + r], rrecv.at[8 + r], y_peer(r))

    def ag_y(r):
        return remote(r2, r3.at[tile(y)], rsend.at[16 + r], rrecv.at[16 + r], y_peer(r))

    def ag_z(r):
        return remote(
            r3, router_grad.at[own_half, cols(z, block)], rsend.at[24 + r], rrecv.at[24 + r], z_peer(r)
        )

    def ag_pair():
        return remote(
            router_grad.at[own_half, :], router_grad.at[own_half, :], rsend.at[32], rrecv.at[32], partner
        )

    def router_0():
        for r in range(1, 2 * NZ):
            remote(cnt_src, cnt.at[r], csend.at[r], crecv.at[r], c_peer(r)).wait_recv()
        totals = cnt_src[...]
        for r in range(1, 2 * NZ):
            totals = totals + cnt[r]
        scale = experts / (top * length)
        frac = scale * totals[0:1, :]
        terms = frac * totals[1:2, :] / length
        lane = lax.broadcasted_iota(jnp.int32, (1, 2 * experts), 1)
        bal_a = jnp.sum(jnp.where(lane < experts, terms, 0.0), axis=1, keepdims=True)
        bal_b = jnp.sum(jnp.where(lane >= experts, terms, 0.0), axis=1, keepdims=True)
        balance[...] = jnp.where(lane == 0, bal_a, bal_b)[:, 0:2]
        e_sub = lax.broadcasted_iota(jnp.int32, (experts, 2 * experts), 0)
        e_lane = lax.broadcasted_iota(jnp.int32, (experts, 2 * experts), 1)
        frac_col = jnp.sum(jnp.where(e_lane == e_sub + experts, frac, 0.0), axis=1, keepdims=True)
        aff_b = aff[:, tokens : 2 * tokens]
        chosen_sum = csum[...]
        shares = aff_b / spread[...]
        inner = jnp.zeros((1, tokens), F32)
        for k in range(top):
            value, _ = picked(picks_b, aff_b, k)
            inner = inner + grads[k : k + 1, :] * value
        agrad = jnp.zeros((experts, tokens), F32)
        for k in range(top):
            hit = picks_b[k : k + 1, :] == labels
            cgrad = ROUTE_SCALE * (grads[k : k + 1, :] / chosen_sum - inner / (chosen_sum * chosen_sum))
            agrad = agrad + jnp.where(hit, cgrad, 0.0)
        share_grad = frac_col / length
        agrad = agrad + (share_grad - jnp.sum(share_grad * shares, axis=0, keepdims=True)) / spread[...]
        lg = agrad * aff_b * (1.0 - aff_b)
        logit[...] = lg
        for b in range(d_model // block):
            rp[:, b * block : (b + 1) * block] = dot(
                lg, normed[b, tokens : 2 * tokens, :].astype(F32), NN, HIGH
            )
        rs_pair().start()

    def router_1():
        rs_pair().wait_recv()
        r0[...] = rp[own_half, :] + b0[...]
        for r in range(1, NZ):
            rs_z(r).start()

    def router_2():
        for r in range(1, NZ):
            rs_z(r).wait_recv()
        acc = r0[:, cols(z, block)]
        for r in range(1, NZ):
            acc = acc + b1[r]
        r1[...] = acc
        for r in range(1, NY):
            rs_y(r).start()

    def router_3():
        for r in range(1, NY):
            rs_y(r).wait_recv()
        acc = r1[tile(y)]
        for r in range(1, NY):
            acc = acc + b2[r]
        r2[...] = acc
        r3[tile(y)] = acc
        for r in range(1, NY):
            ag_y(r).start()

    def router_4():
        for r in range(1, NY):
            ag_y(r).wait_recv()
        router_grad[own_half, cols(z, block)] = r3[...]
        for r in range(1, NZ):
            ag_z(r).start()

    def router_5():
        for r in range(1, NZ):
            ag_z(r).wait_recv()
        ag_pair().start()

    router_at = {3: router_0, 5: router_1, 9: router_2, 11: router_3, 14: router_4, 19: router_5}

    n_tile = 256

    def z_rows(zz):
        return pl.ds(pl.multiple_of(zz * block, block), block)

    def g_block(zz):
        lhs = normed[zz]
        for n in range(hidden // n_tile):
            at = slice(n * n_tile, (n + 1) * n_tile)
            gacc[:, at] += dot(lhs, wgu[0, z_rows(zz), at])
            uacc[:, at] += dot(lhs, wgu[1, z_rows(zz), at])

    def make_hidden():
        def body(i, _):
            rows = cols(i, 16)
            v = gacc[rows, :]
            hid[rows, :] = (v * sigmoid(v) * uacc[rows, :]).astype(BF16)
            return 0

        lax.fori_loop(0, tokens // 16, body, 0)

    def out_send(zz):
        return remote(
            out.at[:, z_rows(zz)], arrived.at[:, z_rows(zz)], osend.at[zz], orecv.at[zz], x_next
        )

    def d_block(zz):
        acc = dot(hid[...], wd[:, z_rows(zz)])
        out[:, z_rows(zz)] = (first[:, z_rows(zz)].astype(F32) + acc).astype(BF16)
        out_send(zz).start()
        lhs = returned[:, z_rows(zz)]
        for n in range(hidden // n_tile):
            at = slice(n * n_tile, (n + 1) * n_tile)
            hgrad[:, at] += dot(lhs, wd[at, z_rows(zz)], NT)

    def consume(fn, group):
        @pl.when(group == 0)
        def _():
            fn(z)

        @pl.when((group > 0) & (group < 4))
        def _():
            fn((z + group) % NZ)
            fn((z - group + NZ) % NZ)

        @pl.when(group == 4)
        def _():
            fn((z + 4) % NZ)

    def slot(t, _):
        nz = t - 1

        @pl.when((nz >= 0) & (nz < GZ))
        def _():
            ref = zg_ref(nz, c, sgn)
            remote(ref, ref, zsend.at[nz], zrecv.at[nz], z_next).wait_recv()
            remote(ref, ref, dzsend.at[nz], dzrecv.at[nz], partner).start()

            @pl.when(nz < GZ - 4)
            def _():
                zg_send(nz + 4).start()

            @pl.when(nz == GZ - 4)
            def _():
                zd_send(0).start()

            @pl.when(nz == GZ - 3)
            def _():
                zd_send(1).start()

        @pl.when((nz >= GZ) & (nz < NZP))
        def _():
            n = nz - GZ
            ref = zd_ref(n, c, sgn)
            remote(ref, ref, zsend.at[nz], zrecv.at[nz], z_next).wait_recv()
            remote(ref, ref, dzsend.at[nz], dzrecv.at[nz], partner).start()

            @pl.when(n < DZ - 2)
            def _():
                zd_send(n + 2).start()

        ndz = t - 3

        @pl.when((ndz >= 0) & (ndz < GZ))
        def _():
            ref = zg_ref(ndz, 1 - c, -sgn)
            remote(ref, ref, dzsend.at[ndz], dzrecv.at[ndz], partner).wait_recv()

        @pl.when((ndz >= GZ) & (ndz < NZP))
        def _():
            ref = zd_ref(ndz - GZ, 1 - c, -sgn)
            remote(ref, ref, dzsend.at[ndz], dzrecv.at[ndz], partner).wait_recv()

        nyr = t - LA - LB * hops

        @pl.when((nyr >= 0) & (nyr < GY))
        def _():
            ref = yg_ref(nyr, c, sgn, 1 - h)
            remote(ref, ref, ysend.at[nyr], yrecv.at[nyr], y_next).wait_recv()
            remote(ref, ref, dysend.at[nyr], dyrecv.at[nyr], partner).start()

        @pl.when((nyr >= GY) & (nyr < NYP))
        def _():
            ref = yd_ref(nyr - GY, c, sgn, 1 - h)
            remote(ref, ref, ysend.at[nyr], yrecv.at[nyr], y_next).wait_recv()
            remote(ref, ref, dysend.at[nyr], dyrecv.at[nyr], partner).start()

        nys = jnp.where(is_last, t - 1, nyr)
        low = jnp.where(is_last, 2, 0)

        @pl.when((nys >= low) & (nys < GY))
        def _():
            yg_send(nys).start()

        @pl.when((nys >= GY) & (nys < NYP))
        def _():
            yd_send(nys - GY).start()

        nyd = t - LA - LB * hops_max - 1

        @pl.when((nyd >= 0) & (nyd < GY))
        def _():
            ref = yg_ref(nyd, 1 - c, -sgn, 1 - h)
            remote(ref, ref, dysend.at[nyd], dyrecv.at[nyd], partner).wait_recv()

            @pl.when((nyd % 4 == 1) | (nyd == GY - 1))
            def _():
                consume(g_block, (nyd + 1) // 4)

            @pl.when(nyd == GY - 1)
            def _():
                make_hidden()

        @pl.when((nyd >= GY) & (nyd < NYP))
        def _():
            n = nyd - GY
            ref = yd_ref(n, 1 - c, -sgn, 1 - h)
            remote(ref, ref, dysend.at[nyd], dyrecv.at[nyd], partner).wait_recv()

            @pl.when(n == 0)
            def _():
                back.wait_recv()

            @pl.when((n % 2 == 0) | (n == DY - 1))
            def _():
                consume(d_block, (n + 1) // 2)

        for at, stage in router_at.items():

            @pl.when(t == at)
            def _():
                stage()

        return 0

    lax.fori_loop(0, NYP + LA + LB * 4 + 1, slot, 0)

    def shared_back(i, _):
        rows = cols(i, 16)
        b_rows = pl.ds(pl.multiple_of(tokens + i * 16, 16), 16)
        v, u, hg = gacc[b_rows, :], uacc[b_rows, :], hgrad[rows, :]
        s = sigmoid(v)
        gg[rows, :] = (hg * u * (s * (1.0 + v * (1.0 - s)))).astype(BF16)
        ug[rows, :] = (hg * v * s).astype(BF16)
        return 0

    lax.fori_loop(0, tokens // 16, shared_back, 0)
    lg_t = jnp.transpose(logit[...])

    def grad_block(b, mean):
        at = z_rows(b)
        grad = dot(gg[...], wgu[0, at, :], NT) + dot(ug[...], wgu[1, at, :], NT)
        grad = grad + dot(lg_t, router_w[:, at], NN, HIGH)
        q = grad * gain[:, at]
        qbuf[b] = q
        return mean + jnp.sum(q * second[:, at].astype(F32), axis=-1, keepdims=True)

    mean = lax.fori_loop(0, d_model // block, grad_block, jnp.zeros((tokens, 1), F32)) / d_model
    inv_b = inverse[tokens : 2 * tokens, 0:1]
    factor = inv_b * inv_b * mean

    def final_block(b, _):
        at = z_rows(b)
        values = second[:, at].astype(F32)
        part = inv_b * (qbuf[b] - values * factor)
        input_grad[:, at] = (returned[:, at].astype(F32) + part).astype(BF16)
        return 0

    lax.fori_loop(0, d_model // block, final_block, 0)

    ag_pair().wait_recv()

    def drain(count, body):
        def step(n, _):
            body(n)
            return 0

        lax.fori_loop(0, count, step, 0)

    drain(2 * NZ // 2, lambda n: out_send(n).wait())
    drain(GZ, lambda n: zg_send(n).wait_send())
    drain(DZ, lambda n: zd_send(n).wait_send())
    drain(GY, lambda n: yg_send(n).wait_send())
    drain(DY, lambda n: yd_send(n).wait_send())

    def pair_done(ref, send, recv):
        remote(ref, ref, send, recv, partner).wait_send()

    drain(GZ, lambda n: pair_done(zg_ref(n, c, sgn), dzsend.at[n], dzrecv.at[n]))
    drain(DZ, lambda n: pair_done(zd_ref(n, c, sgn), dzsend.at[GZ + n], dzrecv.at[GZ + n]))
    drain(GY, lambda n: pair_done(yg_ref(n, c, sgn, 1 - h), dysend.at[n], dyrecv.at[n]))
    drain(DY, lambda n: pair_done(yd_ref(n, c, sgn, 1 - h), dysend.at[GY + n], dyrecv.at[GY + n]))
    back.wait_send()
    for r in range(1, 2 * NZ):
        remote(cnt_src, cnt.at[r], csend.at[r], crecv.at[r], c_peer(r)).wait_send()
    rs_pair().wait_send()
    ag_pair().wait_send()
    for r in range(1, NZ):
        rs_z(r).wait_send()
        ag_z(r).wait_send()
    for r in range(1, NY):
        rs_y(r).wait_send()
        ag_y(r).wait_send()


def shards(
    first_input, second_input, upstream, first_picks, second_picks, gate_grads,
    norm_gain, router_weight, gate_weight, up_weight, down_weight,
):
    tokens, d_model = first_input.shape[2:]
    hidden = gate_weight.shape[2]
    experts = router_weight.shape[1]
    top = first_picks.shape[3]
    block = d_model // NZ
    blocks = d_model // block
    vmem = pl.BlockSpec(memory_space=pltpu.VMEM)
    hbm = pl.BlockSpec(memory_space=pl.ANY)
    sem = pltpu.SemaphoreType.DMA
    half = experts // 2
    outs = pl.pallas_call(
        kernel,
        out_shape=(
            jax.ShapeDtypeStruct((tokens, d_model), BF16),
            jax.ShapeDtypeStruct((top, tokens), F32),
            jax.ShapeDtypeStruct((tokens, d_model), BF16),
            jax.ShapeDtypeStruct((experts, d_model), F32),
            jax.ShapeDtypeStruct((1, 2), F32),
        ),
        in_specs=[vmem, vmem, vmem, vmem, vmem, vmem, vmem, vmem, hbm, hbm, hbm],
        out_specs=(vmem,) * 5,
        scratch_shapes=[
            pltpu.VMEM((2, d_model, hidden), BF16),
            pltpu.VMEM((hidden, d_model), BF16),
            pltpu.VMEM((tokens, d_model), BF16),
            pltpu.VMEM((blocks, 2 * tokens, block), BF16),
            pltpu.VMEM((2 * tokens, 128), F32),
            pltpu.VMEM((2 * tokens, hidden), F32),
            pltpu.VMEM((2 * tokens, hidden), F32),
            pltpu.VMEM((tokens, hidden), F32),
            pltpu.VMEM((tokens, hidden), BF16),
            pltpu.VMEM((tokens, hidden), BF16),
            pltpu.VMEM((tokens, hidden), BF16),
            pltpu.VMEM((tokens, d_model), BF16),
            pltpu.VMEM((blocks, tokens, block), F32),
            pltpu.VMEM((8, 2 * experts), F32),
            pltpu.VMEM((2 * NZ, 8, 2 * experts), F32),
            pltpu.VMEM((experts, 2 * tokens), F32),
            pltpu.VMEM((1, tokens), F32),
            pltpu.VMEM((1, tokens), F32),
            pltpu.VMEM((experts, tokens), F32),
            pltpu.VMEM((experts, d_model), F32),
            pltpu.VMEM((half, d_model), F32),
            pltpu.VMEM((half, d_model), F32),
            pltpu.VMEM((NZ, half, block), F32),
            pltpu.VMEM((half, block), F32),
            pltpu.VMEM((NY, 8, 128), F32),
            pltpu.VMEM((8, 128), F32),
            pltpu.VMEM((half, block), F32),
            sem((3,)),
            sem((NZP,)), sem((NZP,)), sem((NYP,)), sem((NYP,)),
            sem((NZP,)), sem((NZP,)), sem((NYP,)), sem((NYP,)),
            sem((2,)), sem((NZ,)), sem((NZ,)),
            sem((2 * NZ,)), sem((2 * NZ,)), sem((33,)), sem((33,)),
        ],
        compiler_params=pltpu.CompilerParams(
            collective_id=0, has_side_effects=True, vmem_limit_bytes=60 * 1024 * 1024
        ),
    )(
        first_input[0, 0],
        second_input[0, 0],
        upstream[0, 0],
        first_picks[0, 0].T,
        second_picks[0, 0].T,
        gate_grads[0, 0].T,
        norm_gain,
        router_weight[0],
        gate_weight[0],
        up_weight[0],
        down_weight[0],
    )
    arrived, routing, input_grad, router_grad, balance = outs
    return (
        arrived[None, None],
        routing.T[None, None],
        input_grad[None, None],
        router_grad[None],
        balance[None],
    )


def solution(mesh):
    split = Mesh(
        mesh.devices.reshape(mesh.shape["section"], NZ, 2, mesh.shape["dp"]),
        ("section", "ctx_0", "ctx_1", "dp"),
    )
    tokens = P("section", "dp", CTX, None)
    return jax.shard_map(
        shards,
        mesh=split,
        in_specs=(tokens,) * 6
        + (
            P("section", None),
            P("section", None, None),
            P("section", CTX, None),
            P("section", CTX, None),
            P("section", None, CTX),
        ),
        out_specs=(tokens,) * 3 + (P("section", None, None), P("section", "dp", None)),
        check_vma=False,
    )
```

time: 404 us -> 117 us (0.29)
  waiting for transfers between devices: 313 us -> 0 us
  Pallas kernels: 0 us -> 108 us
  starting transfers between devices: 21.7 us -> 0 us
  matrix products: 21.6 us -> 0 us
  blocking collectives: 16.5 us -> 0 us
  between operations: 15.8 us -> 0.67 us
  other arithmetic: 7.71 us -> 0 us
    all_gather x2 -> x0, waiting for transfers between devices: 260 us -> none  [the longest x1 216 us: sent_together(): lax.all_gather(both, axis, axis=dim, tiled=True)]
    pallas_call x0 -> x1, Pallas kernels: none -> 108 us  [shards(): pl.pallas_call(kernel, out_shape=(jax.ShapeDtypeStruct((tokens, d_model),...]
    psum x1 -> x0, waiting for transfers between devices: 41.1 us -> none  [shards(): router_total = lax.psum(router_part, CTX_DP)]
    dot_general x10 -> x0, matrix products: 21.6 us -> none  [the longest x1 4.35 us: shards(): jnp.einsum('td,fd->tf', returned, columns, preferred_element_type=jnp.flo...]
    all_gather x1 -> x0, blocking collectives: 16.5 us -> none  [gather_axes(): array = lax.all_gather(array, axis, axis=dim, tiled=True)]
    all_to_all x1 -> x0, starting transfers between devices: 15.1 us -> none  [sent_to_all(): lax.all_to_all(jnp.broadcast_to(array[None], (size, *array.shape)), axis,...]
    ppermute x2 -> x0, waiting for transfers between devices: 6.72 us -> none  [shifted(): return lax.ppermute(block, axis, route)]
    ppermute x2 -> x0, starting transfers between devices: 6.41 us -> none  [shifted(): return lax.ppermute(block, axis, route)]
  transfers between devices with their start and end apart: 6 -> 0, of which waited for: 5 -> 0; matrix products, arithmetic and copies ran while one was open for 8% -> 0% of each run, Pallas kernels for 0% -> 0%
where the time goes in v1:
time: 117 us; the launch traced here: 116 us
  Pallas kernels  108 us (92%)
  local copies, waits for them, and re-layouts  7.7 us (7%)
    pallas_call x1, Pallas kernels, shards(): pl.pallas_call(kernel, out_shape=(jax.ShapeDtypeStruct((tokens, d_model),...  108 us
    unnamed x20, local copies, waits for them, and re-layouts  7.11 us

profile of v1, /device:TPU:57, one launch (start us, length us, event | category | flops | bytes accessed | tf_op | source)
XLA Modules:
  0.0 116.2 jit_solution(11602900922143455954)
XLA Ops:
  0.6 0.0 copy-start.3
  0.6 0.7 copy-done.3
  1.3 0.0 copy-start.4
  1.3 0.0 copy-start.5
  1.3 0.6 copy.23
  1.9 0.1 copy-done.4
  2.0 0.0 copy-done.5
  2.0 0.6 copy_bitcast_fusion.1
  2.6 107.8 %shard_map.146 = (bf16[128,2048]{1,0:T(8,128)(2,1)}, f32[6,128]{1,0:T(8,128)}, bf16[128,2048]{1,0:T(8,128)(2,1)}, f32[64,2048]{1,0:T(8,128)}, f32[1,2]{1,0:T(1,128)}) custom-call(bf16[128,2048]{1,0:T(8,128)(2,1)} %bitcast.30, bf16[128,2048]{1,0:T(8,128)(2,1)} %bitcast.31, bf16[128,2048]{1,0:T(8,128)(2,1)} %bitcast.32, s32[6,128]{1,0:T(8,128)} %get-tuple-element.21.picks_a, ...), custom_call_target="tpu_custom_call" | custom-call | tf_op jit(solution)/shard_map/pallas_call | solution.py:588
  110.5 0.0 copy-start.2
  110.5 0.7 copy-done.2
  111.2 0.6 copy.16
  111.7 0.0 copy-start.1
  111.7 1.9 %copy.28 = bf16[1,1,128,2048]{3,2,1,0:T(8,128)(2,1)} copy(bf16[1,1,128,2048]{3,2,1,0:T(8,128)(2,1)} %bitcast.29) | data formatting | bytes 1048576
  113.7 0.0 copy-done.1
  113.7 0.0 copy-start
  113.7 0.8 copy.29
  114.5 0.4 copy-done
  114.9 0.0 copy-start.6
  114.9 0.8 copy.30
  115.7 0.0 copy-done.6
  115.7 0.5 copy.31
Async XLA Ops:
  0.6 0.7 copy-start.3
  1.3 0.7 copy-start.4
  1.3 0.7 copy-start.5
  110.5 0.7 copy-start.2
  111.7 1.9 %copy-start.1 = (bf16[128,2048]{1,0:T(8,128)(2,1)S(1)}, bf16[128,2048]{1,0:T(8,128)(2,1)}, u32[]{:S(2)}) copy-start(bf16[128,2048]{1,0:T(8,128)(2,1)} %get-tuple-element.12) | copy-start | bytes 1572868
  113.7 1.2 %copy-start = (f32[64,2048]{1,0:T(8,128)S(1)}, f32[64,2048]{1,0:T(8,128)}, u32[]{:S(2)}) copy-start(f32[64,2048]{1,0:T(8,128)} %get-tuple-element.13) | copy-start | bytes 1572868
  114.9 0.8 copy-start.6

commit v2 on v1

v2 whole, which is shorter than its diff:
```python
import jax
import jax.numpy as jnp
from jax import lax
from jax.experimental import pallas as pl
from jax.experimental.pallas import tpu as pltpu
from jax.sharding import Mesh
from jax.sharding import PartitionSpec as P

CTX = ("ctx_0", "ctx_1")
MESH = pl.DeviceIdType.MESH
EPSILON = 1e-06
ROUTE_SCALE = 2.5
HIGH = lax.Precision.HIGHEST
F32 = jnp.float32
BF16 = jnp.bfloat16

NZ, NY, NX = 8, 8, 4
G, D = 0, 1
Z_ORDER = (
    [(G, 1, m) for m in range(4)]
    + [(G, 2, m) for m in range(4)]
    + [(D, 1, m) for m in range(2)]
    + [(G, 3, m) for m in range(4)]
    + [(D, 2, m) for m in range(2)]
    + [(G, 4, m) for m in range(2)]
    + [(D, 3, m) for m in range(2)]
    + [(D, 4, 0)]
)
Y_ORDER = [(G, 0, 0), (G, 0, 1), (D, 0, 0)]
for _q in ((G, 1), (G, 2), (G, 3), (G, 4), (D, 1), (D, 2), (G, 5), (G, 6), (D, 3), (D, 4), (G, 7), (D, 5), (D, 6), (D, 7)):
    Y_ORDER += [(_q[0], _q[1], m) for m in range(2 - _q[0])]
NZP, NYP = len(Z_ORDER), len(Y_ORDER)
Y_START = 3
LA, LB = 1, 2


def lookup(values, i):
    out = jnp.int32(values[0])
    for p in range(1, len(values)):
        if values[p] != values[p - 1]:
            out = jnp.where(i >= p, jnp.int32(values[p]), out)
    return out


def code(kind, k, m):
    return kind * 64 + k * 4 + m


def z_next_place(entry):
    kind, k, m = entry
    return Z_ORDER.index((kind, k + 1, m)) if (kind, k + 1, m) in Z_ORDER else -1

NT = (((1,), (1,)), ((), ()))
TN = (((0,), (0,)), ((), ()))
NN = (((1,), (0,)), ((), ()))


def dot(a, b, dims=NN, precision=None):
    return lax.dot_general(a, b, dims, precision=precision, preferred_element_type=F32)


def exact_dot(a, b, dims):
    rows = a.shape[0]
    one = a.astype(BF16)
    left = a - one.astype(F32)
    two = left.astype(BF16)
    three = (left - two.astype(F32)).astype(BF16)
    parts = dot(jnp.concatenate([one, two, three], axis=0), b, dims)
    return parts[2 * rows :] + parts[rows : 2 * rows] + parts[:rows]


def sigmoid(v):
    return jax.nn.sigmoid(v)


def kernel(
    first_hbm, second_hbm, upstream, picks_a, picks_b, grads, gain, router_hbm, gate, up, down,
    arrived, routing, input_grad, router_grad, balance,
    first, second, router_w, grad_out, routing_out, balance_out, wgu, wd, returned, normed, inverse, gacc, uacc, hgrad, hid, gg, ug, out, qbuf,
    cnt_src, cnt, aff, csum, spread, logit,
    rp, r0, b0, b1, r1, b2, r2, r3,
    local_sem, zsend, zrecv, ysend, yrecv, dzsend, dzrecv, dysend, dyrecv,
    xsem, osend, orecv, csend, crecv, rsend, rrecv,
):
    d_model = gate.shape[0] * 2 * NZ
    hidden = gate.shape[1]
    tokens = first_hbm.shape[0]
    rows_s = gate.shape[0]
    pg, pd = rows_s // 4, hidden // 2
    block = 2 * rows_s
    length = tokens * 2 * NZ

    x = lax.axis_index("section")
    z = lax.axis_index("ctx_0")
    h = lax.axis_index("ctx_1")
    dp = lax.axis_index("dp")
    j = dp // 2
    c = dp % 2
    y = h * 4 + j
    sgn = 1 - 2 * c

    def dev(xx, zz, yy, cc):
        return (xx, zz, yy // 4, (yy % 4) * 2 + cc)

    partner = dev(x, z, y, 1 - c)
    z_next = dev(x, (z + sgn + NZ) % NZ, y, c)
    z_prev = dev(x, (z - sgn + NZ) % NZ, y, c)
    y_next = dev(x, z, (y + sgn + NY) % NY, c)
    x_next = dev((x + 1) % NX, z, y, c)
    x_prev = dev((x + NX - 1) % NX, z, y, c)

    def z_peer(r):
        return dev(x, (z + r) % NZ, y, c)

    def y_peer(r):
        return dev(x, z, (y + r) % NY, c)

    def c_peer(r):
        rank = (z * 2 + h + r) % (2 * NZ)
        return (x, rank // 2, rank % 2, dp)

    def remote(src, dst, send, recv, device):
        return pltpu.make_async_remote_copy(
            src_ref=src, dst_ref=dst, send_sem=send, recv_sem=recv, device_id=device, device_id_type=MESH
        )

    barrier = pltpu.get_barrier_semaphore()

    def greet(device):
        pl.semaphore_signal(barrier, inc=1, device_id=device, device_id_type=MESH)

    greet(partner)
    greet(x_next)
    greet(x_prev)
    for r in range(1, 2 * NZ):
        greet(c_peer(r))
    for r in range(1, NY):
        if r != 4:
            greet(y_peer(r))

    own = z * 2 + h
    own_rows = pl.ds(pl.multiple_of(own * rows_s, rows_s), rows_s)
    local = [
        pltpu.make_async_copy(first_hbm, first, local_sem.at[0]),
        pltpu.make_async_copy(second_hbm, second, local_sem.at[1]),
        pltpu.make_async_copy(router_hbm, router_w, local_sem.at[2]),
        pltpu.make_async_copy(gate, wgu.at[0, own_rows, :], local_sem.at[3]),
        pltpu.make_async_copy(up, wgu.at[1, own_rows, :], local_sem.at[4]),
        pltpu.make_async_copy(down, wd.at[:, own_rows], local_sem.at[5]),
    ]
    for copy in local:
        copy.start()

    def g_piece(slot, p):
        start = pl.multiple_of(slot * rows_s + p * pg, pg)
        return wgu.at[:, pl.ds(start, pg), :]

    def d_piece(slot, p):
        return wd.at[pl.ds(pl.multiple_of(p * pd, pd), pd), pl.ds(pl.multiple_of(slot * rows_s, rows_s), rows_s)]

    def slot_of(zz, hh):
        return ((zz + 2 * NZ) % NZ) * 2 + hh

    def z_ref(kind, k, m, core, sign):
        slot = slot_of(z - sign * k, h)
        if kind == G:
            return g_piece(slot, (2 * core + m) % 4)
        return d_piece(slot, (core + m) % 2)

    def y_ref(kind, q, m, core, sign, hh):
        slot = slot_of(z + (1 - 2 * (q % 2)) * ((q + 1) // 2) * sign, hh)
        if kind == G:
            return g_piece(slot, 2 * core + m)
        return d_piece(slot, core)

    def z_copy(ref, place):
        return remote(ref, ref, zsend.at[place], zrecv.at[place], z_next)

    def y_copy(ref, place):
        return remote(ref, ref, ysend.at[place], yrecv.at[place], y_next)

    def dz_copy(ref, place):
        return remote(ref, ref, dzsend.at[place], dzrecv.at[place], partner)

    def dy_copy(ref, place):
        return remote(ref, ref, dysend.at[place], dyrecv.at[place], partner)

    last = 3 * (1 - c)
    is_last = j == last
    hops = jnp.where(c == 0, j + 1, 4 - j)
    hops_max = jnp.maximum(hops, 5 - hops)
    send_half = jnp.where(is_last, h, 1 - h)

    step_rows = 16

    def norm_rows(source, base):
        def body(i, _):
            rows = pl.ds(pl.multiple_of(i * step_rows, step_rows), step_rows)
            values = source[rows, :].astype(F32)
            inv = lax.rsqrt(jnp.mean(values * values, axis=-1, keepdims=True) + EPSILON)
            inverse[pl.ds(pl.multiple_of(base + i * step_rows, step_rows), step_rows), :] = jnp.broadcast_to(inv, (step_rows, 128))
            scaled = (values * inv * gain[...]).astype(BF16)
            for b in range(d_model // block):
                normed[b, pl.ds(pl.multiple_of(base + i * step_rows, step_rows), step_rows), :] = scaled[:, b * block : (b + 1) * block]
            return 0

        lax.fori_loop(0, tokens // step_rows, body, 0)

    with jax.named_scope("s_norm"):
        local[0].wait()
        norm_rows(first, 0)
        local[1].wait()
        norm_rows(second, tokens)
    gacc[...] = jnp.zeros_like(gacc)
    uacc[...] = jnp.zeros_like(uacc)
    hgrad[...] = jnp.zeros_like(hgrad)

    experts = router_w.shape[0]
    top = picks_a.shape[1]
    local[2].wait()
    logits = jnp.zeros((experts, 2 * tokens), F32)
    for b in range(d_model // block):
        logits = logits + exact_dot(router_w[:, b * block : (b + 1) * block], normed[b], NT)
    affinity = sigmoid(logits)
    aff[...] = affinity
    labels = lax.broadcasted_iota(jnp.int32, (experts, tokens), 0)

    def picked(picks, affinities, k):
        hit = picks[0, k] == labels
        return jnp.sum(jnp.where(hit, affinities, 0.0), axis=0, keepdims=True), hit

    stats = []
    for m, picks in enumerate((picks_a, picks_b)):
        part = affinity[:, m * tokens : (m + 1) * tokens]
        tab = jnp.zeros((experts, tokens), F32)
        chosen = []
        for k in range(top):
            value, hit = picked(picks, part, k)
            chosen.append(value)
            tab = tab + jnp.where(hit, 1.0, 0.0)
        total = chosen[0]
        for value in chosen[1:]:
            total = total + value
        all_aff = jnp.sum(part, axis=0, keepdims=True)
        if m == 0:
            for k in range(top):
                routing_out[0, k] = ROUTE_SCALE * chosen[k] / total
        else:
            csum[...] = total
            spread[...] = all_aff
        stats.append((tab, part / all_aff))
    ones = jnp.ones((8, tokens), F32)
    counts_row = dot(ones, jnp.concatenate([stats[0][0], stats[1][0]], axis=0), NT, HIGH)
    shares_row = dot(ones, jnp.concatenate([stats[0][1], stats[1][1]], axis=0), NT, HIGH)
    row_id = lax.broadcasted_iota(jnp.int32, (8, 2 * experts), 0)
    packed = jnp.where(row_id == 0, counts_row, jnp.where(row_id == 1, shares_row, 0.0))
    cnt_src[...] = packed
    for copy in local[3:]:
        copy.wait()
    with jax.named_scope("s_barrier"):
        pl.semaphore_wait(barrier, 3 + 2 * NZ - 1 + NY - 2)

    for r in range(1, 2 * NZ):
        remote(cnt_src, cnt.at[r], csend.at[r], crecv.at[r], c_peer(r)).start()
    for m in range(4):
        z_copy(z_ref(G, 0, m, c, sgn), m).start()

    @pl.when(is_last)
    def _():
        for place in range(Y_START):
            y_copy(y_ref(*Y_ORDER[place], c, sgn, send_half), place).start()

    back = remote(upstream, returned, xsem.at[0], xsem.at[1], x_prev)
    back.start()

    half_e = experts // 2
    own_half = pl.ds(pl.multiple_of(c * half_e, half_e), half_e)
    other_half = pl.ds(pl.multiple_of((1 - c) * half_e, half_e), half_e)

    def cols(i, width):
        return pl.ds(pl.multiple_of(i * width, width), width)

    def rs_pair():
        return remote(rp.at[other_half, :], b0, rsend.at[0], rrecv.at[0], partner)

    def part(i):
        return r0.at[:, cols((z + sgn * (i + 1) + 2 * NZ) % NZ, block)]

    def ring(i, source):
        return remote(source, b1.at[i], rsend.at[1 + i], rrecv.at[1 + i], z_prev)

    def tile(yy):
        return (cols(yy // 2, 8), cols(yy % 2, 128))

    def rs_y(r):
        return remote(r1.at[tile((y + r) % NY)], b2.at[r], rsend.at[8 + r], rrecv.at[8 + r], y_peer(r))

    def ag_y(r):
        return remote(r2, r3.at[tile(y)], rsend.at[16 + r], rrecv.at[16 + r], y_peer(r))

    def ag_z(r):
        return remote(
            r3, router_grad.at[own_half, cols(z, block)], rsend.at[24 + r], rrecv.at[24 + r], z_peer(r)
        )

    def ag_pair():
        return remote(
            router_grad.at[own_half, :], router_grad.at[own_half, :], rsend.at[32], rrecv.at[32], partner
        )

    def router_0():
        for r in range(1, 2 * NZ):
            remote(cnt_src, cnt.at[r], csend.at[r], crecv.at[r], c_peer(r)).wait_recv()
        totals = cnt_src[...]
        for r in range(1, 2 * NZ):
            totals = totals + cnt[r]
        scale = experts / (top * length)
        frac = scale * totals[0:1, :]
        terms = frac * totals[1:2, :] / length
        lane = lax.broadcasted_iota(jnp.int32, (1, 2 * experts), 1)
        bal_a = jnp.sum(jnp.where(lane < experts, terms, 0.0), axis=1, keepdims=True)
        bal_b = jnp.sum(jnp.where(lane >= experts, terms, 0.0), axis=1, keepdims=True)
        balance_out[0] = jnp.where(lane == 0, bal_a, bal_b)[:, 0:2]
        e_sub = lax.broadcasted_iota(jnp.int32, (experts, 2 * experts), 0)
        e_lane = lax.broadcasted_iota(jnp.int32, (experts, 2 * experts), 1)
        frac_col = jnp.sum(jnp.where(e_lane == e_sub + experts, frac, 0.0), axis=1, keepdims=True)
        aff_b = aff[:, tokens : 2 * tokens]
        chosen_sum = csum[...]
        shares = aff_b / spread[...]
        inner = jnp.zeros((1, tokens), F32)
        for k in range(top):
            value, _ = picked(picks_b, aff_b, k)
            inner = inner + grads[0, k] * value
        agrad = jnp.zeros((experts, tokens), F32)
        for k in range(top):
            hit = picks_b[0, k] == labels
            cgrad = ROUTE_SCALE * (grads[0, k] / chosen_sum - inner / (chosen_sum * chosen_sum))
            agrad = agrad + jnp.where(hit, cgrad, 0.0)
        share_grad = frac_col / length
        agrad = agrad + (share_grad - jnp.sum(share_grad * shares, axis=0, keepdims=True)) / spread[...]
        lg = agrad * aff_b * (1.0 - aff_b)
        logit[...] = lg
        for b in range(d_model // block):
            rp[:, b * block : (b + 1) * block] = exact_dot(lg, normed[b, tokens : 2 * tokens, :], NN)
        rs_pair().start()

    def router_term():
        lg_t = jnp.transpose(logit[...])
        for b in range(d_model // block):
            at = slice(b * block, (b + 1) * block)
            qbuf[b] = dot(lg_t, router_w[:, at], NN, HIGH)

    def router_1():
        rs_pair().wait_recv()
        r0[...] = rp[own_half, :] + b0[...]
        ring(0, part(0)).start()

    def ring_step(i):
        ring(i - 1, b1.at[i - 1]).wait_recv()
        b1[i - 1] = b1[i - 1] + part(i)[...]

        @pl.when(i < NZ - 1)
        def _():
            ring(i, b1.at[i - 1]).start()

        @pl.when(i == NZ - 1)
        def _():
            r1[...] = b1[i - 1]
            for r in range(1, NY):
                rs_y(r).start()

    def router_3():
        for r in range(1, NY):
            rs_y(r).wait_recv()
        acc = r1[tile(y)]
        for r in range(1, NY):
            acc = acc + b2[r]
        r2[...] = acc
        r3[tile(y)] = acc
        for r in range(1, NY):
            ag_y(r).start()

    def router_4():
        for r in range(1, NY):
            ag_y(r).wait_recv()
        pltpu.make_async_copy(r3, router_grad.at[own_half, cols(z, block)], local_sem.at[1]).start()
        for r in range(1, NZ):
            ag_z(r).start()

    def router_5():
        for r in range(1, NZ):
            ag_z(r).wait_recv()
        pltpu.make_async_copy(r3, router_grad.at[own_half, cols(z, block)], local_sem.at[1]).wait()
        ag_pair().start()

    router_at = {4: router_0, 5: router_1, 7: router_term, 23: router_3, 26: router_4, 32: router_5}
    ring_at, ring_every = 5, 2

    n_tile = 256

    def z_rows(zz):
        return pl.ds(pl.multiple_of(zz * block, block), block)

    def g_block(zz):
        lhs = normed[zz]
        for n in range(hidden // n_tile):
            at = slice(n * n_tile, (n + 1) * n_tile)
            gacc[:, at] += dot(lhs, wgu[0, z_rows(zz), at])
            uacc[:, at] += dot(lhs, wgu[1, z_rows(zz), at])

    def make_hidden():
        def body(i, _):
            rows = cols(i, 16)
            v = gacc[rows, :]
            hid[rows, :] = (v * sigmoid(v) * uacc[rows, :]).astype(BF16)
            return 0

        lax.fori_loop(0, tokens // 16, body, 0)

    def out_send(zz):
        return remote(
            out.at[:, z_rows(zz)], arrived.at[:, z_rows(zz)], osend.at[zz], orecv.at[zz], x_next
        )

    def out_block(zz):
        acc = dot(hid[...], wd[:, z_rows(zz)])
        out[:, z_rows(zz)] = (first[:, z_rows(zz)].astype(F32) + acc).astype(BF16)
        out_send(zz).start()

    def hgrad_block(zz):
        lhs = returned[:, z_rows(zz)]
        for n in range(hidden // n_tile):
            at = slice(n * n_tile, (n + 1) * n_tile)
            hgrad[:, at] += dot(lhs, wd[at, z_rows(zz)], NT)

    def pair(fn, group):
        fn((z + group) % NZ)
        fn((z - group + NZ) % NZ)

    def on_g(q):
        @pl.when(q == 0)
        def _():
            g_block(z)

        @pl.when((q % 2 == 0) & (q > 0))
        def _():
            pair(g_block, q // 2)

        @pl.when(q == NZ - 1)
        def _():
            g_block((z + 4) % NZ)
            make_hidden()

            def body(i, _):
                out_block((z + i + NZ - 2) % NZ)
                return 0

            lax.fori_loop(0, 5, body, 0)

    def on_d(q):
        @pl.when(q == 0)
        def _():
            back.wait_recv()
            hgrad_block(z)

        @pl.when((q % 2 == 0) & (q > 0))
        def _():
            pair(hgrad_block, q // 2)

        @pl.when(q == 6)
        def _():
            pair(out_block, 3)

        @pl.when(q == NZ - 1)
        def _():
            out_block((z + 4) % NZ)
            hgrad_block((z + 4) % NZ)

    z_codes = [code(*entry) for entry in Z_ORDER]
    y_codes = [code(*entry) for entry in Y_ORDER]
    z_follow = [z_next_place(entry) for entry in Z_ORDER]
    d1 = Z_ORDER.index((D, 1, 0))
    g2_end = 3

    def by_kind(entry, fn):
        for kind in (G, D):

            @pl.when(entry // 64 == kind)
            def _():
                fn(kind, (entry % 64) // 4, entry % 4)

    def slot(t, _):
        nz = t - 1

        @pl.when((nz >= 0) & (nz < NZP))
        def _():
            follow = lookup(z_follow, nz)

            def arrived_z(kind, k, m):
                ref = z_ref(kind, k, m, c, sgn)
                with jax.named_scope("w_z"):
                    z_copy(ref, nz).wait_recv()

                @pl.when(follow >= 0)
                def _():
                    z_copy(ref, follow).start()

                dz_copy(ref, nz).start()

            by_kind(lookup(z_codes, nz), arrived_z)

            @pl.when(nz == g2_end)
            def _():
                for m in range(2):
                    z_copy(z_ref(D, 0, m, c, sgn), d1 + m).start()

        ndz = t - 2

        @pl.when((ndz >= 0) & (ndz < NZP))
        def _():
            def arrived_dz(kind, k, m):
                with jax.named_scope("w_dz"):
                    dz_copy(z_ref(kind, k, m, 1 - c, -sgn), ndz).wait_recv()

            by_kind(lookup(z_codes, ndz), arrived_dz)

        nyr = t - LA - LB * hops

        @pl.when((nyr >= 0) & (nyr < NYP))
        def _():
            def arrived_y(kind, q, m):
                ref = y_ref(kind, q, m, c, sgn, 1 - h)
                with jax.named_scope("w_y"):
                    y_copy(ref, nyr).wait_recv()

                @pl.when(jnp.logical_not(is_last))
                def _():
                    y_copy(ref, nyr).start()

                dy_copy(ref, nyr).start()

            by_kind(lookup(y_codes, nyr), arrived_y)

        nys = t + 1

        @pl.when(is_last & (nys >= Y_START) & (nys < NYP))
        def _():
            def inject(kind, q, m):
                y_copy(y_ref(kind, q, m, c, sgn, h), nys).start()

            by_kind(lookup(y_codes, nys), inject)

        nyd = t - LA - LB * hops_max - 1

        @pl.when((nyd >= 0) & (nyd < NYP))
        def _():
            def arrived_dy(kind, q, m):
                with jax.named_scope("w_dy"):
                    dy_copy(y_ref(kind, q, m, 1 - c, -sgn, 1 - h), nyd).wait_recv()
                if kind == G:

                    @pl.when(m == 1)
                    def _():
                        with jax.named_scope("c_g"):
                            on_g(q)

                else:
                    with jax.named_scope("c_d"):
                        on_d(q)

            by_kind(lookup(y_codes, nyd), arrived_dy)

        ring_i = (t - ring_at) // ring_every

        @pl.when((t > ring_at) & ((t - ring_at) % ring_every == 0) & (ring_i < NZ))
        def _():
            with jax.named_scope("ring_step"):
                ring_step(ring_i)

        for at, stage in router_at.items():

            @pl.when(t == at)
            def _():
                with jax.named_scope(stage.__name__):
                    stage()

        return 0

    lax.fori_loop(0, NYP + LA + LB * 4 + 1, slot, 0)

    def shared_back(i, _):
        rows = cols(i, 16)
        b_rows = pl.ds(pl.multiple_of(tokens + i * 16, 16), 16)
        v, u, hg = gacc[b_rows, :], uacc[b_rows, :], hgrad[rows, :]
        s = sigmoid(v)
        gg[rows, :] = (hg * u * (s * (1.0 + v * (1.0 - s)))).astype(BF16)
        ug[rows, :] = (hg * v * s).astype(BF16)
        return 0

    with jax.named_scope("t_back"):
        lax.fori_loop(0, tokens // 16, shared_back, 0)
    def grad_block(b, mean):
        at = z_rows(b)
        grad = dot(gg[...], wgu[0, at, :], NT) + dot(ug[...], wgu[1, at, :], NT)
        q = (grad + qbuf[b]) * gain[:, at]
        qbuf[b] = q
        return mean + jnp.sum(q * second[:, at].astype(F32), axis=-1, keepdims=True)

    with jax.named_scope("t_grad"):
        mean = lax.fori_loop(0, d_model // block, grad_block, jnp.zeros((tokens, 1), F32)) / d_model
    inv_b = inverse[tokens : 2 * tokens, 0:1]
    factor = inv_b * inv_b * mean

    def final_block(b, _):
        at = z_rows(b)
        values = second[:, at].astype(F32)
        part = inv_b * (qbuf[b] - values * factor)
        grad_out[:, at] = (returned[:, at].astype(F32) + part).astype(BF16)
        return 0

    with jax.named_scope("t_final"):
        lax.fori_loop(0, d_model // block, final_block, 0)

    with jax.named_scope("t_agpair"):
        ag_pair().wait_recv()
    results = [
        pltpu.make_async_copy(grad_out, input_grad, local_sem.at[0]),
        pltpu.make_async_copy(routing_out, routing, local_sem.at[2]),
        pltpu.make_async_copy(balance_out, balance, local_sem.at[3]),
    ]
    for result in results:
        result.start()

    def drain(count, body):
        def step(n, _):
            body(n)
            return 0

        lax.fori_loop(0, count, step, 0)

    with jax.named_scope("t_out"):
        drain(2 * NZ // 2, lambda n: out_send(n).wait())
    for order, copies in ((Z_ORDER, (z_copy, dz_copy)), (Y_ORDER, (y_copy, dy_copy))):
        for place, entry in enumerate(order):
            ref = g_piece(0, 0) if entry[0] == G else d_piece(0, 0)
            for copy in copies:
                copy(ref, place).wait_send()
    back.wait_send()
    for r in range(1, 2 * NZ):
        remote(cnt_src, cnt.at[r], csend.at[r], crecv.at[r], c_peer(r)).wait_send()
    rs_pair().wait_send()
    ag_pair().wait_send()
    for r in range(1, NZ):
        ring(r - 1, b1.at[0]).wait_send()
        ag_z(r).wait_send()
    for r in range(1, NY):
        rs_y(r).wait_send()
        ag_y(r).wait_send()
    for result in results:
        result.wait()


def leave(*refs):
    n = (len(refs) - 1) // 3
    sems = refs[-1]
    into = [pltpu.make_async_copy(refs[i], refs[2 * n + i], sems.at[0, i]) for i in range(n)]
    away = [pltpu.make_async_copy(refs[2 * n + i], refs[n + i], sems.at[1, i]) for i in range(n)]
    for copy in into:
        copy.start()
    for i in range(n):
        into[i].wait()
        away[i].start()
    for copy in away:
        copy.wait()


def shards(
    first_input, second_input, upstream, first_picks, second_picks, gate_grads,
    norm_gain, router_weight, gate_weight, up_weight, down_weight,
):
    tokens, d_model = first_input.shape[2:]
    hidden = gate_weight.shape[2]
    experts = router_weight.shape[1]
    top = first_picks.shape[3]
    block = d_model // NZ
    blocks = d_model // block
    vmem = pl.BlockSpec(memory_space=pltpu.VMEM)
    hbm = pl.BlockSpec(memory_space=pltpu.HBM)
    anywhere = pl.BlockSpec(memory_space=pl.ANY)
    sem = pltpu.SemaphoreType.DMA
    half = experts // 2
    outs = pl.pallas_call(
        kernel,
        out_shape=(
            jax.ShapeDtypeStruct((tokens, d_model), BF16),
            jax.ShapeDtypeStruct((1, top, 1, tokens), F32),
            jax.ShapeDtypeStruct((tokens, d_model), BF16),
            jax.ShapeDtypeStruct((experts, d_model), F32),
            jax.ShapeDtypeStruct((1, 1, 2), F32),
        ),
        in_specs=[hbm, hbm, hbm, vmem, vmem, vmem, vmem, hbm, hbm, hbm, hbm],
        out_specs=(anywhere,) * 5,
        scratch_shapes=[
            pltpu.VMEM((tokens, d_model), BF16),
            pltpu.VMEM((tokens, d_model), BF16),
            pltpu.VMEM((experts, d_model), F32),
            pltpu.VMEM((tokens, d_model), BF16),
            pltpu.VMEM((1, top, 1, tokens), F32),
            pltpu.VMEM((1, 1, 2), F32),
            pltpu.VMEM((2, d_model, hidden), BF16),
            pltpu.VMEM((hidden, d_model), BF16),
            pltpu.VMEM((tokens, d_model), BF16),
            pltpu.VMEM((blocks, 2 * tokens, block), BF16),
            pltpu.VMEM((2 * tokens, 128), F32),
            pltpu.VMEM((2 * tokens, hidden), F32),
            pltpu.VMEM((2 * tokens, hidden), F32),
            pltpu.VMEM((tokens, hidden), F32),
            pltpu.VMEM((tokens, hidden), BF16),
            pltpu.VMEM((tokens, hidden), BF16),
            pltpu.VMEM((tokens, hidden), BF16),
            pltpu.VMEM((tokens, d_model), BF16),
            pltpu.VMEM((blocks, tokens, block), F32),
            pltpu.VMEM((8, 2 * experts), F32),
            pltpu.VMEM((2 * NZ, 8, 2 * experts), F32),
            pltpu.VMEM((experts, 2 * tokens), F32),
            pltpu.VMEM((1, tokens), F32),
            pltpu.VMEM((1, tokens), F32),
            pltpu.VMEM((experts, tokens), F32),
            pltpu.VMEM((experts, d_model), F32),
            pltpu.VMEM((half, d_model), F32),
            pltpu.VMEM((half, d_model), F32),
            pltpu.VMEM((NZ, half, block), F32),
            pltpu.VMEM((half, block), F32),
            pltpu.VMEM((NY, 8, 128), F32),
            pltpu.VMEM((8, 128), F32),
            pltpu.VMEM((half, block), F32),
            sem((6,)),
            sem((NZP,)), sem((NZP,)), sem((NYP,)), sem((NYP,)),
            sem((NZP,)), sem((NZP,)), sem((NYP,)), sem((NYP,)),
            sem((2,)), sem((NZ,)), sem((NZ,)),
            sem((2 * NZ,)), sem((2 * NZ,)), sem((33,)), sem((33,)),
        ],
        compiler_params=pltpu.CompilerParams(
            collective_id=0, has_side_effects=True, vmem_limit_bytes=62 * 1024 * 1024
        ),
    )(
        first_input[0, 0],
        second_input[0, 0],
        upstream[0, 0],
        jnp.transpose(first_picks, (0, 3, 1, 2)),
        jnp.transpose(second_picks, (0, 3, 1, 2)),
        jnp.transpose(gate_grads, (0, 3, 1, 2)),
        norm_gain,
        router_weight[0],
        gate_weight[0],
        up_weight[0],
        down_weight[0],
    )
    arrived, routing, input_grad, router_grad, balance = pl.pallas_call(
        leave,
        out_shape=tuple(jax.ShapeDtypeStruct(a.shape, a.dtype) for a in outs),
        in_specs=[anywhere] * 5,
        out_specs=(hbm,) * 5,
        scratch_shapes=[pltpu.VMEM(a.shape, a.dtype) for a in outs] + [sem((2, 5))],
    )(*outs)
    return (
        arrived[None, None],
        jnp.transpose(routing, (0, 2, 3, 1)),
        input_grad[None, None],
        router_grad[None],
        balance,
    )


def solution(mesh):
    split = Mesh(
        mesh.devices.reshape(mesh.shape["section"], NZ, 2, mesh.shape["dp"]),
        ("section", "ctx_0", "ctx_1", "dp"),
    )
    tokens = P("section", "dp", CTX, None)
    return jax.shard_map(
        shards,
        mesh=split,
        in_specs=(tokens,) * 6
        + (
            P("section", None),
            P("section", None, None),
            P("section", CTX, None),
            P("section", CTX, None),
            P("section", None, CTX),
        ),
        out_specs=(tokens,) * 3 + (P("section", None, None), P("section", "dp", None)),
        check_vma=False,
    )
```

time: 117 us -> 98.9 us (0.85)
  Pallas kernels: 108 us -> 97.3 us
  local copies, waits for them, and re-layouts: 7.7 us -> 0 us
    pallas_call x1, Pallas kernels: 108 us -> 95 us  [shards(): pl.pallas_call(kernel, out_shape=(jax.ShapeDtypeStruct((tokens, d_model),...]
    unnamed x20 -> x0, local copies, waits for them, and re-layouts: 7.11 us -> none
    pallas_call x0 -> x1, Pallas kernels: none -> 2.27 us  [shards(): pl.pallas_call(leave, out_shape=tuple((jax.ShapeDtypeStruct(a.shape, a.dt...]
where the time goes in v2:
time: 98.9 us; the launch traced here: 98 us
  Pallas kernels  97.3 us (98%)
    pallas_call x1, Pallas kernels, shards(): pl.pallas_call(kernel, out_shape=(jax.ShapeDtypeStruct((tokens, d_model),...  95 us
    pallas_call x1, Pallas kernels, shards(): pl.pallas_call(leave, out_shape=tuple((jax.ShapeDtypeStruct(a.shape, a.dt...  2.27 us

profile of v2, /device:TPU:57, one launch (start us, length us, event | category | flops | bytes accessed | tf_op | source)
XLA Modules:
  0.0 98.0 jit_solution(1026597360912646823)
XLA Ops:
  0.6 95.0 %shard_map.146 = (bf16[128,2048]{1,0:T(8,128)(2,1)}, f32[1,6,1,128]{3,2,1,0:T(1,128)}, bf16[128,2048]{1,0:T(8,128)(2,1)}, f32[64,2048]{1,0:T(8,128)}, f32[1,1,2]{2,1,0:T(1,128)}) custom-call(bf16[128,2048]{1,0:T(8,128)(2,1)} %bitcast.14, bf16[128,2048]{1,0:T(8,128)(2,1)} %bitcast.15, bf16[128,2048]{1,0:T(8,128)(2,1)} %bitcast.16, s32[1,6,1,128]{3,2,1,0:T(1,128)} %bitcast.21, ...), custom_call_target="tpu_custom_call" | custom-call | tf_op jit(solution)/shard_map/pallas_call | solution.py:692
  95.7 2.3 %shard_map.147 = (bf16[128,2048]{1,0:T(8,128)(2,1)}, f32[1,6,1,128]{3,2,1,0:T(1,128)}, bf16[128,2048]{1,0:T(8,128)(2,1)}, f32[64,2048]{1,0:T(8,128)}, f32[1,1,2]{2,1,0:T(1,128)}) custom-call(bf16[128,2048]{1,0:T(8,128)(2,1)} %get-tuple-element.15.refs_0_, f32[1,6,1,128]{3,2,1,0:T(1,128)} %get-tuple-element.16.refs_1_, ...), custom_call_target="tpu_custom_call" | custom-call | tf_op jit(solution)/shard_map/pallas_call | solution.py:759

commit v3 on v2

--- a/solution.py
+++ b/solution.py
@@ -27,9 +27,13 @@
     + [(D, 4, 0)]
 )
 Y_ORDER = [(G, 0, 0), (G, 0, 1), (D, 0, 0)]
-for _q in ((G, 1), (G, 2), (G, 3), (G, 4), (D, 1), (D, 2), (G, 5), (G, 6), (D, 3), (D, 4), (G, 7), (D, 5), (D, 6), (D, 7)):
+for _q in ((G, 1), (G, 2), (G, 3), (G, 4), (D, 1), (D, 2), (G, 5), (G, 6), (D, 3), (D, 4)):
     Y_ORDER += [(_q[0], _q[1], m) for m in range(2 - _q[0])]
 NZP, NYP = len(Z_ORDER), len(Y_ORDER)
+E_ORDER = [(G, 4, 0), (G, 4, 0), (D, 3, 0), (D, 3, 1), (D, 4, 0)]
+NE = len(E_ORDER)
+G5, D3, D4 = Y_ORDER.index((G, 5, 0)), Y_ORDER.index((D, 3, 0)), Y_ORDER.index((D, 4, 0))
+E_LAG = 2
 Y_START = 3
 LA, LB = 1, 2
 
@@ -104,7 +108,7 @@
 
     partner = dev(x, z, y, 1 - c)
     z_next = dev(x, (z + sgn + NZ) % NZ, y, c)
-    z_prev = dev(x, (z - sgn + NZ) % NZ, y, c)
+    y_prev = dev(x, z, (y - sgn + NY) % NY, c)
     y_next = dev(x, z, (y + sgn + NY) % NY, c)
     x_next = dev((x + 1) % NX, z, y, c)
     x_prev = dev((x + NX - 1) % NX, z, y, c)
@@ -172,6 +176,13 @@
         if kind == G:
             return g_piece(slot, 2 * core + m)
         return d_piece(slot, core)
+
+    def e_ref(i, core, sign):
+        kind, k, flip = E_ORDER[i]
+        slot = slot_of(z - sign * k, 1 - h)
+        if kind == G:
+            return g_piece(slot, 2 * core + i)
+        return d_piece(slot, (core + flip) % 2)
 
     def z_copy(ref, place):
         return remote(ref, ref, zsend.at[place], zrecv.at[place], z_next)
@@ -284,23 +295,23 @@
         return remote(rp.at[other_half, :], b0, rsend.at[0], rrecv.at[0], partner)
 
     def part(i):
-        return r0.at[:, cols((z + sgn * (i + 1) + 2 * NZ) % NZ, block)]
+        return r0.at[:, cols((y + sgn * (i + 1) + 2 * NY) % NY, block)]
 
     def ring(i, source):
-        return remote(source, b1.at[i], rsend.at[1 + i], rrecv.at[1 + i], z_prev)
+        return remote(source, b1.at[i], rsend.at[1 + i], rrecv.at[1 + i], y_prev)
 
     def tile(yy):
         return (cols(yy // 2, 8), cols(yy % 2, 128))
 
-    def rs_y(r):
-        return remote(r1.at[tile((y + r) % NY)], b2.at[r], rsend.at[8 + r], rrecv.at[8 + r], y_peer(r))
-
-    def ag_y(r):
-        return remote(r2, r3.at[tile(y)], rsend.at[16 + r], rrecv.at[16 + r], y_peer(r))
-
-    def ag_z(r):
+    def rs_small(r):
+        return remote(r1.at[tile((z + r) % NZ)], b2.at[r], rsend.at[8 + r], rrecv.at[8 + r], z_peer(r))
+
+    def ag_small(r):
+        return remote(r2, r3.at[tile(z)], rsend.at[16 + r], rrecv.at[16 + r], z_peer(r))
+
+    def ag_big(r):
         return remote(
-            r3, router_grad.at[own_half, cols(z, block)], rsend.at[24 + r], rrecv.at[24 + r], z_peer(r)
+            r3, router_grad.at[own_half, cols(y, block)], rsend.at[24 + r], rrecv.at[24 + r], y_peer(r)
         )
 
     def ag_pair():
@@ -367,34 +378,32 @@
         def _():
             r1[...] = b1[i - 1]
             for r in range(1, NY):
-                rs_y(r).start()
+                rs_small(r).start()
 
     def router_3():
         for r in range(1, NY):
-            rs_y(r).wait_recv()
-        acc = r1[tile(y)]
+            rs_small(r).wait_recv()
+        acc = r1[tile(z)]
         for r in range(1, NY):
             acc = acc + b2[r]
         r2[...] = acc
-        r3[tile(y)] = acc
+        r3[tile(z)] = acc
         for r in range(1, NY):
-            ag_y(r).start()
+            ag_small(r).start()
 
     def router_4():
         for r in range(1, NY):
-            ag_y(r).wait_recv()
-        pltpu.make_async_copy(r3, router_grad.at[own_half, cols(z, block)], local_sem.at[1]).start()
-        for r in range(1, NZ):
-            ag_z(r).start()
+            ag_small(r).wait_recv()
+        pltpu.make_async_copy(r3, router_grad.at[own_half, cols(y, block)], local_sem.at[1]).start()
 
     def router_5():
         for r in range(1, NZ):
-            ag_z(r).wait_recv()
-        pltpu.make_async_copy(r3, router_grad.at[own_half, cols(z, block)], local_sem.at[1]).wait()
+            ag_big(r).wait_recv()
+        pltpu.make_async_copy(r3, router_grad.at[own_half, cols(y, block)], local_sem.at[1]).wait()
         ag_pair().start()
 
-    router_at = {4: router_0, 5: router_1, 7: router_term, 23: router_3, 26: router_4, 32: router_5}
-    ring_at, ring_every = 5, 2
+    router_at = {4: router_0, 5: router_1, 7: router_term, 22: router_3, 25: router_4}
+    ring_at, ring_every, spread_at = 5, 2, 25
 
     n_tile = 256
 
@@ -446,16 +455,15 @@
         def _():
             pair(g_block, q // 2)
 
-        @pl.when(q == NZ - 1)
-        def _():
-            g_block((z + 4) % NZ)
-            make_hidden()
-
-            def body(i, _):
-                out_block((z + i + NZ - 2) % NZ)
-                return 0
-
-            lax.fori_loop(0, 5, body, 0)
+    def all_g():
+        g_block((z + 4) % NZ)
+        make_hidden()
+
+        def body(i, _):
+            out_block((z + i + NZ - 1) % NZ)
+            return 0
+
+        lax.fori_loop(0, 3, body, 0)
 
     def on_d(q):
         @pl.when(q == 0)
@@ -467,14 +475,15 @@
         def _():
             pair(hgrad_block, q // 2)
 
-        @pl.when(q == 6)
-        def _():
-            pair(out_block, 3)
-
-        @pl.when(q == NZ - 1)
-        def _():
-            out_block((z + 4) % NZ)
-            hgrad_block((z + 4) % NZ)
+        @pl.when(q == 4)
+        def _():
+            pair(out_block, 2)
+
+    def all_d():
+        pair(hgrad_block, 3)
+        hgrad_block((z + 4) % NZ)
+        pair(out_block, 3)
+        out_block((z + 4) % NZ)
 
     z_codes = [code(*entry) for entry in Z_ORDER]
     y_codes = [code(*entry) for entry in Y_ORDER]
@@ -538,8 +547,38 @@
                     y_copy(ref, nyr).start()
 
                 dy_copy(ref, nyr).start()
+                if kind == G:
+
+                    @pl.when(q == 5)
+                    def _():
+                        z_copy(ref, NZP + m).start()
+
+                else:
+
+                    @pl.when(q == 3)
+                    def _():
+                        z_copy(ref, NZP + 2).start()
 
             by_kind(lookup(y_codes, nyr), arrived_y)
+
+        def arrived_e(i):
+            ref = e_ref(i, c, sgn)
+            with jax.named_scope("w_e"):
+                z_copy(ref, NZP + i).wait_recv()
+            if i == 2:
+                z_copy(ref, NZP + 4).start()
+            dz_copy(ref, NZP + i).start()
+
+        def arrived_de(i):
+            with jax.named_scope("w_de"):
+                dz_copy(e_ref(i, 1 - c, -sgn), NZP + i).wait_recv()
+
+        late = t - LA - LB * hops_max
+        for i, place in ((0, G5), (1, G5 + 1), (2, D3), (4, D3 + E_LAG)):
+
+            @pl.when(late == place + E_LAG)
+            def _():
+                arrived_e(i)
 
         nys = t + 1
 
@@ -565,10 +604,39 @@
                             on_g(q)
 
                 else:
+                    @pl.when(q == 4)
+                    def _():
+                        z_copy(y_ref(kind, q, m, 1 - c, -sgn, 1 - h), NZP + 3).start()
+
                     with jax.named_scope("c_d"):
                         on_d(q)
 
             by_kind(lookup(y_codes, nyd), arrived_dy)
+
+        @pl.when(nyd == G5 + E_LAG)
+        def _():
+            arrived_de(0)
+
+        @pl.when(nyd == G5 + 1 + E_LAG)
+        def _():
+            arrived_de(1)
+            with jax.named_scope("c_allg"):
+                all_g()
+
+        @pl.when(nyd == D3 + E_LAG)
+        def _():
+            arrived_de(2)
+
+        @pl.when(nyd == D4 + E_LAG)
+        def _():
+            arrived_e(3)
+
+        @pl.when(nyd == D4 + E_LAG + 1)
+        def _():
+            arrived_de(3)
+            arrived_de(4)
+            with jax.named_scope("c_alld"):
+                all_d()
 
         ring_i = (t - ring_at) // ring_every
 
@@ -584,9 +652,19 @@
                 with jax.named_scope(stage.__name__):
                     stage()
 
+        spread_i = t - spread_at
+
+        @pl.when((spread_i >= 0) & (spread_i < 4))
+        def _():
+            ag_big(4 + spread_i).start()
+
+            @pl.when(spread_i < 3)
+            def _():
+                ag_big(3 - spread_i).start()
+
         return 0
 
-    lax.fori_loop(0, NYP + LA + LB * 4 + 1, slot, 0)
+    lax.fori_loop(0, D4 + E_LAG + 2 + LA + LB * 4 + 1, slot, 0)
 
     def shared_back(i, _):
         rows = cols(i, 16)
@@ -606,8 +684,10 @@
         qbuf[b] = q
         return mean + jnp.sum(q * second[:, at].astype(F32), axis=-1, keepdims=True)
 
+    with jax.named_scope("router_5"):
+        router_5()
     with jax.named_scope("t_grad"):
-        mean = lax.fori_loop(0, d_model // block, grad_block, jnp.zeros((tokens, 1), F32)) / d_model
+        mean = lax.fori_loop(0, d_model // block, grad_block, jnp.zeros((tokens, 1), F32), unroll=True) / d_model
     inv_b = inverse[tokens : 2 * tokens, 0:1]
     factor = inv_b * inv_b * mean
 
@@ -640,7 +720,7 @@
 
     with jax.named_scope("t_out"):
         drain(2 * NZ // 2, lambda n: out_send(n).wait())
-    for order, copies in ((Z_ORDER, (z_copy, dz_copy)), (Y_ORDER, (y_copy, dy_copy))):
+    for order, copies in ((Z_ORDER + E_ORDER, (z_copy, dz_copy)), (Y_ORDER, (y_copy, dy_copy))):
         for place, entry in enumerate(order):
             ref = g_piece(0, 0) if entry[0] == G else d_piece(0, 0)
             for copy in copies:
@@ -652,10 +732,10 @@
     ag_pair().wait_send()
     for r in range(1, NZ):
         ring(r - 1, b1.at[0]).wait_send()
-        ag_z(r).wait_send()
+        ag_big(r).wait_send()
     for r in range(1, NY):
-        rs_y(r).wait_send()
-        ag_y(r).wait_send()
+        rs_small(r).wait_send()
+        ag_small(r).wait_send()
     for result in results:
         result.wait()
 
@@ -735,8 +815,8 @@
             pltpu.VMEM((8, 128), F32),
             pltpu.VMEM((half, block), F32),
             sem((6,)),
-            sem((NZP,)), sem((NZP,)), sem((NYP,)), sem((NYP,)),
-            sem((NZP,)), sem((NZP,)), sem((NYP,)), sem((NYP,)),
+            sem((NZP + NE,)), sem((NZP + NE,)), sem((NYP,)), sem((NYP,)),
+            sem((NZP + NE,)), sem((NZP + NE,)), sem((NYP,)), sem((NYP,)),
             sem((2,)), sem((NZ,)), sem((NZ,)),
             sem((2 * NZ,)), sem((2 * NZ,)), sem((33,)), sem((33,)),
         ],

time: 98.9 us -> 99.8 us (level)
  no operation moved by 1% of the time
where the time goes in v3:
time: 99.8 us; the launch traced here: 98.1 us
  Pallas kernels  97.5 us (98%)
    pallas_call x1, Pallas kernels, shards(): pl.pallas_call(kernel, out_shape=(jax.ShapeDtypeStruct((tokens, d_model),...  95.2 us
    pallas_call x1, Pallas kernels, shards(): pl.pallas_call(leave, out_shape=tuple((jax.ShapeDtypeStruct(a.shape, a.dt...  2.27 us

profile of v3, /device:TPU:57, one launch (start us, length us, event | category | flops | bytes accessed | tf_op | source)
XLA Modules:
  0.0 98.1 jit_solution(12716033159680172454)
XLA Ops:
  0.6 95.2 %shard_map.146 = (bf16[128,2048]{1,0:T(8,128)(2,1)}, f32[1,6,1,128]{3,2,1,0:T(1,128)}, bf16[128,2048]{1,0:T(8,128)(2,1)}, f32[64,2048]{1,0:T(8,128)}, f32[1,1,2]{2,1,0:T(1,128)}) custom-call(bf16[128,2048]{1,0:T(8,128)(2,1)} %bitcast.14, bf16[128,2048]{1,0:T(8,128)(2,1)} %bitcast.15, bf16[128,2048]{1,0:T(8,128)(2,1)} %bitcast.16, s32[1,6,1,128]{3,2,1,0:T(1,128)} %bitcast.21, ...), custom_call_target="tpu_custom_call" | custom-call | tf_op jit(solution)/shard_map/pallas_call | solution.py:772
  95.9 2.3 %shard_map.147 = (bf16[128,2048]{1,0:T(8,128)(2,1)}, f32[1,6,1,128]{3,2,1,0:T(1,128)}, bf16[128,2048]{1,0:T(8,128)(2,1)}, f32[64,2048]{1,0:T(8,128)}, f32[1,1,2]{2,1,0:T(1,128)}) custom-call(bf16[128,2048]{1,0:T(8,128)(2,1)} %get-tuple-element.15.refs_0_, f32[1,6,1,128]{3,2,1,0:T(1,128)} %get-tuple-element.16.refs_1_, ...), custom_call_target="tpu_custom_call" | custom-call | tf_op jit(solution)/shard_map/pallas_call | solution.py:839

commit v4 on v3

--- a/solution.py
+++ b/solution.py
@@ -35,7 +35,10 @@
 G5, D3, D4 = Y_ORDER.index((G, 5, 0)), Y_ORDER.index((D, 3, 0)), Y_ORDER.index((D, 4, 0))
 E_LAG = 2
 Y_START = 3
-LA, LB = 1, 2
+
+
+def lag(hops):
+    return 1 + 5 * hops // 2
 
 
 def lookup(values, i):
@@ -81,7 +84,7 @@
     first_hbm, second_hbm, upstream, picks_a, picks_b, grads, gain, router_hbm, gate, up, down,
     arrived, routing, input_grad, router_grad, balance,
     first, second, router_w, grad_out, routing_out, balance_out, wgu, wd, returned, normed, inverse, gacc, uacc, hgrad, hid, gg, ug, out, qbuf,
-    cnt_src, cnt, aff, csum, spread, logit,
+    cnt_src, cnt_sum, cnt, aff, csum, spread, logit,
     rp, r0, b0, b1, r1, b2, r2, r3,
     local_sem, zsend, zrecv, ysend, yrecv, dzsend, dzrecv, dysend, dyrecv,
     xsem, osend, orecv, csend, crecv, rsend, rrecv,
@@ -119,9 +122,11 @@
     def y_peer(r):
         return dev(x, z, (y + r) % NY, c)
 
-    def c_peer(r):
-        rank = (z * 2 + h + r) % (2 * NZ)
-        return (x, rank // 2, rank % 2, dp)
+    def count_z(r):
+        return remote(cnt_src, cnt.at[r], csend.at[r], crecv.at[r], z_peer(r))
+
+    def count_y():
+        return remote(cnt_sum, cnt.at[0], csend.at[0], crecv.at[0], y_peer(NY // 2))
 
     def remote(src, dst, send, recv, device):
         return pltpu.make_async_remote_copy(
@@ -136,11 +141,10 @@
     greet(partner)
     greet(x_next)
     greet(x_prev)
-    for r in range(1, 2 * NZ):
-        greet(c_peer(r))
+    for r in range(1, NZ):
+        greet(z_peer(r))
     for r in range(1, NY):
-        if r != 4:
-            greet(y_peer(r))
+        greet(y_peer(r))
 
     own = z * 2 + h
     own_rows = pl.ds(pl.multiple_of(own * rows_s, rows_s), rows_s)
@@ -152,7 +156,7 @@
         pltpu.make_async_copy(up, wgu.at[1, own_rows, :], local_sem.at[4]),
         pltpu.make_async_copy(down, wd.at[:, own_rows], local_sem.at[5]),
     ]
-    for copy in local:
+    for copy in local[3:] + local[:3]:
         copy.start()
 
     def g_piece(slot, p):
@@ -201,6 +205,21 @@
     hops = jnp.where(c == 0, j + 1, 4 - j)
     hops_max = jnp.maximum(hops, 5 - hops)
     send_half = jnp.where(is_last, h, 1 - h)
+
+    for copy in local[3:]:
+        copy.wait()
+    with jax.named_scope("s_barrier"):
+        pl.semaphore_wait(barrier, 3 + NZ - 1 + NY - 1)
+    for m in range(3):
+        z_copy(z_ref(G, 0, m, c, sgn), m).start()
+
+    @pl.when(is_last)
+    def _():
+        for place in range(Y_START):
+            y_copy(y_ref(*Y_ORDER[place], c, sgn, send_half), place).start()
+
+    back = remote(upstream, returned, xsem.at[0], xsem.at[1], x_prev)
+    back.start()
 
     step_rows = 16
 
@@ -266,23 +285,9 @@
     row_id = lax.broadcasted_iota(jnp.int32, (8, 2 * experts), 0)
     packed = jnp.where(row_id == 0, counts_row, jnp.where(row_id == 1, shares_row, 0.0))
     cnt_src[...] = packed
-    for copy in local[3:]:
-        copy.wait()
-    with jax.named_scope("s_barrier"):
-        pl.semaphore_wait(barrier, 3 + 2 * NZ - 1 + NY - 2)
-
-    for r in range(1, 2 * NZ):
-        remote(cnt_src, cnt.at[r], csend.at[r], crecv.at[r], c_peer(r)).start()
-    for m in range(4):
-        z_copy(z_ref(G, 0, m, c, sgn), m).start()
-
-    @pl.when(is_last)
-    def _():
-        for place in range(Y_START):
-            y_copy(y_ref(*Y_ORDER[place], c, sgn, send_half), place).start()
-
-    back = remote(upstream, returned, xsem.at[0], xsem.at[1], x_prev)
-    back.start()
+    for r in range(1, NZ):
+        count_z(r).start()
+    z_copy(z_ref(G, 0, 3, c, sgn), 3).start()
 
     half_e = experts // 2
     own_half = pl.ds(pl.multiple_of(c * half_e, half_e), half_e)
@@ -319,12 +324,18 @@
             router_grad.at[own_half, :], router_grad.at[own_half, :], rsend.at[32], rrecv.at[32], partner
         )
 
+    def router_counts():
+        for r in range(1, NZ):
+            count_z(r).wait_recv()
+        totals = cnt_src[...]
+        for r in range(1, NZ):
+            totals = totals + cnt[r]
+        cnt_sum[...] = totals
+        count_y().start()
+
     def router_0():
-        for r in range(1, 2 * NZ):
-            remote(cnt_src, cnt.at[r], csend.at[r], crecv.at[r], c_peer(r)).wait_recv()
-        totals = cnt_src[...]
-        for r in range(1, 2 * NZ):
-            totals = totals + cnt[r]
+        count_y().wait_recv()
+        totals = cnt_sum[...] + cnt[0]
         scale = experts / (top * length)
         frac = scale * totals[0:1, :]
         terms = frac * totals[1:2, :] / length
@@ -402,8 +413,8 @@
         pltpu.make_async_copy(r3, router_grad.at[own_half, cols(y, block)], local_sem.at[1]).wait()
         ag_pair().start()
 
-    router_at = {4: router_0, 5: router_1, 7: router_term, 22: router_3, 25: router_4}
-    ring_at, ring_every, spread_at = 5, 2, 25
+    router_at = {3: router_counts, 5: router_0, 6: router_1, 8: router_term, 22: router_3, 26: router_4}
+    ring_at, ring_every, spread_at = 6, 2, 27
 
     n_tile = 256
 
@@ -533,7 +544,7 @@
 
             by_kind(lookup(z_codes, ndz), arrived_dz)
 
-        nyr = t - LA - LB * hops
+        nyr = t - lag(hops)
 
         @pl.when((nyr >= 0) & (nyr < NYP))
         def _():
@@ -573,7 +584,7 @@
             with jax.named_scope("w_de"):
                 dz_copy(e_ref(i, 1 - c, -sgn), NZP + i).wait_recv()
 
-        late = t - LA - LB * hops_max
+        late = t - lag(hops_max)
         for i, place in ((0, G5), (1, G5 + 1), (2, D3), (4, D3 + E_LAG)):
 
             @pl.when(late == place + E_LAG)
@@ -589,7 +600,7 @@
 
             by_kind(lookup(y_codes, nys), inject)
 
-        nyd = t - LA - LB * hops_max - 1
+        nyd = t - lag(hops_max) - 1
 
         @pl.when((nyd >= 0) & (nyd < NYP))
         def _():
@@ -664,7 +675,7 @@
 
         return 0
 
-    lax.fori_loop(0, D4 + E_LAG + 2 + LA + LB * 4 + 1, slot, 0)
+    lax.fori_loop(0, D4 + E_LAG + 2 + lag(4) + 1, slot, 0)
 
     def shared_back(i, _):
         rows = cols(i, 16)
@@ -726,8 +737,9 @@
             for copy in copies:
                 copy(ref, place).wait_send()
     back.wait_send()
-    for r in range(1, 2 * NZ):
-        remote(cnt_src, cnt.at[r], csend.at[r], crecv.at[r], c_peer(r)).wait_send()
+    count_y().wait_send()
+    for r in range(1, NZ):
+        count_z(r).wait_send()
     rs_pair().wait_send()
     ag_pair().wait_send()
     for r in range(1, NZ):
@@ -801,7 +813,8 @@
             pltpu.VMEM((tokens, d_model), BF16),
             pltpu.VMEM((blocks, tokens, block), F32),
             pltpu.VMEM((8, 2 * experts), F32),
-            pltpu.VMEM((2 * NZ, 8, 2 * experts), F32),
+            pltpu.VMEM((8, 2 * experts), F32),
+            pltpu.VMEM((NZ, 8, 2 * experts), F32),
             pltpu.VMEM((experts, 2 * tokens), F32),
             pltpu.VMEM((1, tokens), F32),
             pltpu.VMEM((1, tokens), F32),
@@ -818,7 +831,7 @@
             sem((NZP + NE,)), sem((NZP + NE,)), sem((NYP,)), sem((NYP,)),
             sem((NZP + NE,)), sem((NZP + NE,)), sem((NYP,)), sem((NYP,)),
             sem((2,)), sem((NZ,)), sem((NZ,)),
-            sem((2 * NZ,)), sem((2 * NZ,)), sem((33,)), sem((33,)),
+            sem((NZ,)), sem((NZ,)), sem((33,)), sem((33,)),
         ],
         compiler_params=pltpu.CompilerParams(
             collective_id=0, has_side_effects=True, vmem_limit_bytes=62 * 1024 * 1024

time: 99.8 us -> 97.2 us (0.974); the launches traced: 98.1 us -> 97 us
  Pallas kernels: 97.5 us -> 96.3 us
    pallas_call x1, Pallas kernels: 95.2 us -> 94.1 us  [shards(): pl.pallas_call(kernel, out_shape=(jax.ShapeDtypeStruct((tokens, d_model),...]
where the time goes in v4:
time: 97.2 us; the launch traced here: 97 us
  Pallas kernels  96.3 us (99%)
    pallas_call x1, Pallas kernels, shards(): pl.pallas_call(kernel, out_shape=(jax.ShapeDtypeStruct((tokens, d_model),...  94.1 us
    pallas_call x1, Pallas kernels, shards(): pl.pallas_call(leave, out_shape=tuple((jax.ShapeDtypeStruct(a.shape, a.dt...  2.27 us

profile of v4, /device:TPU:57, one launch (start us, length us, event | category | flops | bytes accessed | tf_op | source)
XLA Modules:
  0.0 97.0 jit_solution(14527350228361015059)
XLA Ops:
  0.6 94.1 %shard_map.146 = (bf16[128,2048]{1,0:T(8,128)(2,1)}, f32[1,6,1,128]{3,2,1,0:T(1,128)}, bf16[128,2048]{1,0:T(8,128)(2,1)}, f32[64,2048]{1,0:T(8,128)}, f32[1,1,2]{2,1,0:T(1,128)}) custom-call(bf16[128,2048]{1,0:T(8,128)(2,1)} %bitcast.14, bf16[128,2048]{1,0:T(8,128)(2,1)} %bitcast.15, bf16[128,2048]{1,0:T(8,128)(2,1)} %bitcast.16, s32[1,6,1,128]{3,2,1,0:T(1,128)} %bitcast.21, ...), custom_call_target="tpu_custom_call" | custom-call | tf_op jit(solution)/shard_map/pallas_call | solution.py:784
  94.7 2.3 %shard_map.147 = (bf16[128,2048]{1,0:T(8,128)(2,1)}, f32[1,6,1,128]{3,2,1,0:T(1,128)}, bf16[128,2048]{1,0:T(8,128)(2,1)}, f32[64,2048]{1,0:T(8,128)}, f32[1,1,2]{2,1,0:T(1,128)}) custom-call(bf16[128,2048]{1,0:T(8,128)(2,1)} %get-tuple-element.15.refs_0_, f32[1,6,1,128]{3,2,1,0:T(1,128)} %get-tuple-element.16.refs_1_, ...), custom_call_target="tpu_custom_call" | custom-call | tf_op jit(solution)/shard_map/pallas_call | solution.py:852
